TPU v7x, 16 devices: a whole 2x2x2 slice. The times are simulated.
16 devices in a mesh: dp: 2 (over z), tp: 8 (over y, x, core).
Axes of the slice: x: 2, y: 2, z: 2, core: 2. Of those that a mesh axis runs over, the one named last changes fastest.
Arguments:
- y1: float32 [4, 12, 64, 1664], P('dp'), parts along dimension 0
- y2: float32 [4, 12, 64, 1664], P('dp'), parts along dimension 0
- dy1: float32 [4, 12, 64, 1664], P('dp'), parts along dimension 0
- dy2: float32 [4, 12, 64, 1664], P('dp'), parts along dimension 0
- w_qkv: bfloat16 [3, 1664, 3, 16, 104], P(None, None, None, 'tp')
- w_out: bfloat16 [3, 16, 104, 1664], P(None, 'tp')
- w_up: bfloat16 [3, 1664, 8192], P(None, None, 'tp')
- w_down: bfloat16 [3, 8192, 1664], P(None, 'tp')
Outputs:
- output 1: float32 [4, 12, 64, 1664], P('dp'), parts along dimension 0
- output 2: float32 [4, 12, 64, 1664], P('dp'), parts along dimension 0
- output 3: float32 [4, 12, 64, 1664], P('dp'), parts along dimension 0
- output 4: float32 [4, 12, 64, 1664], P('dp'), parts along dimension 0
- output 5: float32 [6, 1664, 3, 16, 104], P('dp', None, None, 'tp'), parts along dimension 0
- output 6: float32 [6, 16, 104, 1664], P('dp', 'tp'), parts along dimension 0
- output 7: float32 [6, 1664, 8192], P('dp', None, 'tp'), parts along dimension 0
- output 8: float32 [6, 8192, 1664], P('dp', 'tp'), parts along dimension 0
There are 2 independent parts. A program takes and returns all parts, laid end to end along the dimension named above; an argument that names none is the same for every part.
All inputs are finite; a program needn't handle non-finite values.
Results may differ from a plain program's by a relative error of at most 0.0111879.
Values are sent between devices in bfloat16 or wider.
A program may use at most 1 GiB of HBM per device.

v0:
```python
import jax
import jax.numpy as jnp
from jax import lax
from jax.sharding import PartitionSpec as P

EPS = 1e-6


def rms_norm(x_in):
    return x_in * lax.rsqrt(jnp.mean(x_in * x_in, axis=-1, keepdims=True) + EPS)


def norm_back(x_in, grad_norm):
    return jax.vjp(rms_norm, x_in)[1](grad_norm)[0]


def mlp_forward(x_in, w_up, w_down):
    normed = rms_norm(x_in).astype(jnp.bfloat16)
    up_pre = jnp.einsum('rsh,hf->rsf', normed, w_up, preferred_element_type=jnp.float32)
    act_full, gelu_pull = jax.vjp(jax.nn.gelu, up_pre)
    act_half = act_full.astype(jnp.bfloat16)
    part_out = jnp.einsum('rsf,fh->rsh', act_half, w_down, preferred_element_type=jnp.float32)
    return part_out, (normed, act_half, gelu_pull)


def mlp_backward(grad_two, saved_mlp, w_up, w_down):
    normed, act_half, gelu_pull = saved_mlp
    grad_half = grad_two.astype(jnp.bfloat16)
    d_down = jnp.einsum('rsf,rsh->fh', act_half, grad_half, preferred_element_type=jnp.float32)
    d_act = jnp.einsum('rsh,fh->rsf', grad_half, w_down, preferred_element_type=jnp.float32)
    d_pre = gelu_pull(d_act)[0].astype(jnp.bfloat16)
    d_up = jnp.einsum('rsh,rsf->hf', normed, d_pre, preferred_element_type=jnp.float32)
    norm_part = jnp.einsum('rsf,hf->rsh', d_pre, w_up, preferred_element_type=jnp.float32)
    return norm_part, d_up, d_down


def attn_forward(x_in, w_qkv, w_out):
    normed = rms_norm(x_in).astype(jnp.bfloat16)
    qkv_all = jnp.einsum('rsh,hcnd->crsnd', normed, w_qkv, preferred_element_type=jnp.float32).astype(jnp.bfloat16)
    q_heads, k_heads, v_heads = qkv_all[0], qkv_all[1], qkv_all[2]
    att_scale = q_heads.shape[-1] ** -0.5
    scores = jnp.einsum('rqnd,rknd->rnqk', q_heads, k_heads, preferred_element_type=jnp.float32) * att_scale
    prob_full = jax.nn.softmax(scores, axis=-1)
    prob_half = prob_full.astype(jnp.bfloat16)
    attn_out = jnp.einsum('rnqk,rknd->rqnd', prob_half, v_heads, preferred_element_type=jnp.float32).astype(jnp.bfloat16)
    part_out = jnp.einsum('rqnd,ndh->rqh', attn_out, w_out, preferred_element_type=jnp.float32)
    return part_out, (normed, q_heads, k_heads, v_heads, prob_full, prob_half, attn_out)


def attn_backward(grad_one, saved_attn, w_qkv, w_out):
    normed, q_heads, k_heads, v_heads, prob_full, prob_half, attn_out = saved_attn
    att_scale = q_heads.shape[-1] ** -0.5
    grad_half = grad_one.astype(jnp.bfloat16)
    d_wout = jnp.einsum('rqnd,rqh->ndh', attn_out, grad_half, preferred_element_type=jnp.float32)
    d_attn = jnp.einsum('rqh,ndh->rqnd', grad_half, w_out, preferred_element_type=jnp.float32).astype(jnp.bfloat16)
    d_vals = jnp.einsum('rnqk,rqnd->rknd', prob_half, d_attn, preferred_element_type=jnp.float32)
    d_probs = jnp.einsum('rqnd,rknd->rnqk', d_attn, v_heads, preferred_element_type=jnp.float32)
    row_dot = jnp.sum(d_probs * prob_full, axis=-1, keepdims=True)
    d_scores = (prob_full * (d_probs - row_dot) * att_scale).astype(jnp.bfloat16)
    d_query = jnp.einsum('rnqk,rknd->rqnd', d_scores, k_heads, preferred_element_type=jnp.float32)
    d_keys = jnp.einsum('rnqk,rqnd->rknd', d_scores, q_heads, preferred_element_type=jnp.float32)
    d_qkv = jnp.stack([d_query.astype(jnp.bfloat16), d_keys.astype(jnp.bfloat16), d_vals.astype(jnp.bfloat16)])
    d_wqkv = jnp.einsum('rsh,crsnd->hcnd', normed, d_qkv, preferred_element_type=jnp.float32)
    norm_part = jnp.einsum('crsnd,hcnd->rsh', d_qkv, w_qkv, preferred_element_type=jnp.float32)
    return norm_part, d_wqkv, d_wout


def solution(mesh):
    act_spec = P('dp')
    in_specs = (act_spec, act_spec, act_spec, act_spec,
                P(None, None, None, 'tp', None), P(None, 'tp', None, None),
                P(None, None, 'tp'), P(None, 'tp', None))
    out_specs = (act_spec, act_spec, act_spec, act_spec,
                 P('dp', None, None, 'tp', None), P('dp', 'tp', None, None),
                 P('dp', None, 'tp'), P('dp', 'tp', None))

    def device_body(y_one, y_two, dy_one, dy_two, w_qkv, w_out, w_up, w_down):
        n_micro, n_batch, seq_len, model_dim = y_one.shape
        row_shape = (n_micro * n_batch, seq_len, model_dim)
        upper_one = y_one.reshape(row_shape)
        upper_two = y_two.reshape(row_shape)
        grad_one = dy_one.reshape(row_shape)
        grad_two = dy_two.reshape(row_shape)
        grads_qkv, grads_out, grads_up, grads_down = [], [], [], []
        for layer_idx in reversed(range(w_qkv.shape[0])):
            g_part, saved_mlp = mlp_forward(upper_one, w_up[layer_idx], w_down[layer_idx])
            lower_two = upper_two - lax.psum(g_part, 'tp')
            norm_part, d_up, d_down = mlp_backward(grad_two, saved_mlp, w_up[layer_idx], w_down[layer_idx])
            norm_sum = lax.psum(norm_part.astype(jnp.bfloat16), 'tp')
            grad_one = grad_one + norm_back(upper_one, norm_sum.astype(jnp.float32))
            f_part, saved_attn = attn_forward(lower_two, w_qkv[layer_idx], w_out[layer_idx])
            lower_one = upper_one - lax.psum(f_part, 'tp')
            norm_part, d_wqkv, d_wout = attn_backward(grad_one, saved_attn, w_qkv[layer_idx], w_out[layer_idx])
            norm_sum = lax.psum(norm_part.astype(jnp.bfloat16), 'tp')
            grad_two = grad_two + norm_back(lower_two, norm_sum.astype(jnp.float32))
            upper_one, upper_two = lower_one, lower_two
            grads_qkv.append(d_wqkv)
            grads_out.append(d_wout)
            grads_up.append(d_up)
            grads_down.append(d_down)
        return (upper_one.reshape(y_one.shape), upper_two.reshape(y_one.shape),
                grad_one.reshape(y_one.shape), grad_two.reshape(y_one.shape),
                jnp.stack(grads_qkv[::-1]), jnp.stack(grads_out[::-1]),
                jnp.stack(grads_up[::-1]), jnp.stack(grads_down[::-1]))

    return jax.shard_map(device_body, mesh=mesh, in_specs=in_specs, out_specs=out_specs, check_vma=False)
```

profile of v0, /device:TPU:0, one launch (start us, length us, event | category | flops | bytes accessed | tf_op | source)
XLA Modules:
  0.0 1633.2 jit_solution(3610587327736111586)
XLA Ops:
  17.0 8.8 fusion.91
  28.5 11.5 fusion.88
  40.3 10.4 bitcast_convert_fusion.3
  50.8 12.3 fusion.24
  64.7 9.6 convolution_convert_fusion.2
  74.9 106.4 %all-reduce.13.cloned.1.call-done = f32[24,64,1664]{2,1,0:T(8,128)} async-done(((f32[24,64,1664]{2,1,0:T(8,128)}), f32[24,64,1664]{2,1,0:T(8,128)}) %all-reduce.13.cloned.1.call-update) | async-done | bytes 10223632 | tf_op jit(solution)/shard_map/psum | solution.py:87
  181.2 11.9 multiply_reduce_fusion.4
  193.1 8.9 convert_bitcast_fusion.2
  214.3 54.0 %all-reduce.25.cloned.1.call-done = bf16[24,64,1664]{2,1,0:T(8,128)(2,1)} async-done(((bf16[24,64,1664]{2,1,0:T(8,128)(2,1)}), bf16[24,64,1664]{2,1,0:T(8,128)(2,1)}) %all-reduce.25.cloned.1.call-update) | async-done | bytes 5111824 | tf_op jit(solution)/shard_map/psum | solution.py:89
  268.3 142.6 %all-reduce.15.cloned.1.call-done = f32[24,64,1664]{2,1,0:T(8,128)} async-done(((f32[24,64,1664]{2,1,0:T(8,128)}), f32[24,64,1664]{2,1,0:T(8,128)}) %all-reduce.15.cloned.1.call-update) | async-done | bytes 10223632 | tf_op jit(solution)/shard_map/psum | solution.py:92
  410.9 14.5 multiply_reduce_fusion.3
  449.1 8.3 bitcast_convert_fusion.2
  457.7 9.6 fusion.85
  469.9 11.5 fusion.82
  481.8 58.9 %all-reduce.27.cloned.1.call-done = bf16[24,64,1664]{2,1,0:T(8,128)(2,1)} async-done(((bf16[24,64,1664]{2,1,0:T(8,128)(2,1)}), bf16[24,64,1664]{2,1,0:T(8,128)(2,1)}) %all-reduce.27.cloned.1.call-update) | async-done | bytes 5111824 | tf_op jit(solution)/shard_map/psum | solution.py:94
  547.1 136.0 %all-reduce.17.cloned.1.call-done = f32[24,64,1664]{2,1,0:T(8,128)} async-done(((f32[24,64,1664]{2,1,0:T(8,128)}), f32[24,64,1664]{2,1,0:T(8,128)}) %all-reduce.17.cloned.1.call-update) | async-done | bytes 10223632 | tf_op jit(solution)/shard_map/psum | solution.py:87
  683.1 16.7 %multiply_reduce_fusion.2 = (f32[24,64]{1,0:T(8,128)S(1)}, f32[24,64,1664]{2,1,0:T(8,128)}, f32[24,64,1664]{2,1,0:T(8,128)S(1)}) fusion(f32[24,64,1664]{2,1,0:T(8,128)} %get-tuple-element.17, f32[24,64,1664]{2,1,0:T(8,128)} %all-reduce.17.cloned.1.call-done, f32[24,64]{1,0:T(8,128)S(1)} %multiply_multiply_fusion.10, f32[24,64]{1,0:T(8,128)S(1)} %fusion.259, ...), kind=kLoop, calls=%fused_computation.49 | loop fusion | flops 23001600 | bytes 56248320 | tf_op jit(solution)/shard_map/reduce_sum | solution.py:10
  699.8 16.0 fusion.31
  717.4 9.6 convolution_convert_fusion.1
  727.0 11.0 all-reduce.19.cloned.1.call-start
  738.0 8.9 convert_bitcast_fusion.1
  758.9 11.8 convolution_bitcast_fusion.3
  773.2 9.9 fusion.72
  783.2 8.3 fusion.65
  791.5 18.8 %all-reduce.29.cloned.1.call-done = bf16[24,64,1664]{2,1,0:T(8,128)(2,1)} async-done(((bf16[24,64,1664]{2,1,0:T(8,128)(2,1)}), bf16[24,64,1664]{2,1,0:T(8,128)(2,1)}) %all-reduce.29.cloned.1.call-update) | async-done | bytes 5111824 | tf_op jit(solution)/shard_map/psum | solution.py:89
  816.8 136.1 %all-reduce.19.cloned.1.call-done = f32[24,64,1664]{2,1,0:T(8,128)} async-done(((f32[24,64,1664]{2,1,0:T(8,128)}), f32[24,64,1664]{2,1,0:T(8,128)}) %all-reduce.19.cloned.1.call-update) | async-done | bytes 10223632 | tf_op jit(solution)/shard_map/psum | solution.py:92
  952.8 16.7 %multiply_reduce_fusion.1 = (f32[24,64]{1,0:T(8,128)S(1)}, f32[24,64,1664]{2,1,0:T(8,128)}, f32[24,64,1664]{2,1,0:T(8,128)S(1)}) fusion(f32[24,64,1664]{2,1,0:T(8,128)} %get-tuple-element.15, f32[24,64,1664]{2,1,0:T(8,128)} %all-reduce.19.cloned.1.call-done, f32[24,64,1664]{2,1,0:T(8,128)} %copy-done.2, f32[24,64]{1,0:T(8,128)S(1)} %multiply_multiply_fusion.9, ...), kind=kLoop, calls=%fused_computation.47 | loop fusion | flops 23001600 | bytes 56248320 | tf_op jit(solution)/shard_map/reduce_sum | solution.py:10
  981.3 8.4 bitcast_convert_fusion.1
  989.8 9.6 fusion.79
  1002.2 11.5 fusion.76
  1013.8 13.3 convolution_bitcast_fusion.4
  1027.1 11.9 convolution_bitcast_fusion.6
  1045.4 27.7 %all-reduce.31.cloned.1.call-done = bf16[24,64,1664]{2,1,0:T(8,128)(2,1)} async-done(((bf16[24,64,1664]{2,1,0:T(8,128)(2,1)}), bf16[24,64,1664]{2,1,0:T(8,128)(2,1)}) %all-reduce.31.cloned.1.call-update) | async-done | bytes 5111824 | tf_op jit(solution)/shard_map/psum | solution.py:94
  1079.5 136.1 %all-reduce.21.cloned.1.call-done = f32[24,64,1664]{2,1,0:T(8,128)} async-done(((f32[24,64,1664]{2,1,0:T(8,128)}), f32[24,64,1664]{2,1,0:T(8,128)}) %all-reduce.21.cloned.1.call-update) | async-done | bytes 10223632 | tf_op jit(solution)/shard_map/psum | solution.py:87
  1215.6 16.9 %multiply_reduce_fusion = (f32[24,64]{1,0:T(8,128)S(1)}, f32[24,64,1664]{2,1,0:T(8,128)}, f32[24,64,1664]{2,1,0:T(8,128)S(1)}) fusion(f32[24,64,1664]{2,1,0:T(8,128)} %get-tuple-element.13, f32[24,64,1664]{2,1,0:T(8,128)} %all-reduce.21.cloned.1.call-done, f32[24,64,1664]{2,1,0:T(8,128)} %copy-done.3, f32[24,64]{1,0:T(8,128)S(1)} %multiply_multiply_fusion.8, ...), kind=kLoop, calls=%fused_computation.45 | loop fusion | flops 23001600 | bytes 56248320 | tf_op jit(solution)/shard_map/reduce_sum | solution.py:10
  1232.5 15.9 fusion.38
  1250.1 9.7 convolution_convert_fusion
  1266.7 8.6 convert_bitcast_fusion
  1287.4 12.3 convolution_bitcast_fusion.5
  1299.7 16.0 pad_maximum_fusion.1
  1315.8 9.4 convolution_bitcast_fusion.7
  1325.3 10.3 pad_maximum_fusion
  1335.6 7.5 all-reduce.33.cloned.1.call-done
  1349.5 136.1 %all-reduce.23.cloned.1.call-done = f32[24,64,1664]{2,1,0:T(8,128)} async-done(((f32[24,64,1664]{2,1,0:T(8,128)}), f32[24,64,1664]{2,1,0:T(8,128)}) %all-reduce.23.cloned.1.call-update) | async-done | bytes 10223632 | tf_op jit(solution)/shard_map/psum | solution.py:92
  1485.7 16.6 %fusion.16 = (f32[24,64,1664]{2,1,0:T(8,128)S(1)}, f32[24,64,1664]{2,1,0:T(8,128)}) fusion(f32[24,64,1664]{2,1,0:T(8,128)} %copy-done.1, bf16[24,64,1664]{2,1,0:T(8,128)(2,1)} %all-reduce.33.cloned.1.call-done, f32[24,64,1664]{2,1,0:T(8,128)} %get-tuple-element.11, f32[24,64]{1,0:T(8,128)S(1)} %multiply_multiply_fusion.7, f32[24,64]{1,0:T(8,128)S(1)} %copy-done.35, ...), kind=kLoop, calls=%fused_computation.37 | loop fusion | flops 17891328 | bytes 56242176 | tf_op jit(solution)/shard_map/add | solution.py:90
  1515.6 8.4 bitcast_convert_fusion
  1543.1 64.2 %all-reduce.35.cloned.1.call-done = bf16[24,64,1664]{2,1,0:T(8,128)(2,1)} async-done(((bf16[24,64,1664]{2,1,0:T(8,128)(2,1)}), bf16[24,64,1664]{2,1,0:T(8,128)(2,1)}) %all-reduce.35.cloned.1.call-update) | async-done | bytes 5111824 | tf_op jit(solution)/shard_map/psum | solution.py:94
  1614.1 12.0 fusion.17
  (237 shorter events, 176.4 us)
Async XLA Ops:
  7.2 174.1 %all-reduce.13.cloned.1.call-start = ((), (), s32[]{:S(2)}) async-start(), calls=%async_computation | async-start | bytes 20447232 | tf_op jit(solution)/shard_map/psum | solution.py:87
  40.0 228.3 %all-reduce.25.cloned.1.call-start = ((), (), s32[]{:S(2)}) async-start(), calls=%async_computation.6 | async-start | bytes 10223616 | tf_op jit(solution)/shard_map/psum | solution.py:89
  74.3 336.6 %all-reduce.15.cloned.1.call-start = ((), (), s32[]{:S(2)}) async-start(), calls=%async_computation.1 | async-start | bytes 20447232 | tf_op jit(solution)/shard_map/psum | solution.py:92
  214.0 326.6 %all-reduce.27.cloned.1.call-start = ((), (), s32[]{:S(2)}) async-start(), calls=%async_computation.7 | async-start | bytes 10223616 | tf_op jit(solution)/shard_map/psum | solution.py:94
  410.9 14.6 slice-start
  410.9 14.6 slice-start.1
  410.9 14.6 slice-start.2
  410.9 16.5 %copy-start.7 = (bf16[24,64,1664]{2,1,0:T(8,128)(2,1)S(1)}, bf16[24,64,1664]{2,1,0:T(8,128)(2,1)}, u32[]{:S(2)}) copy-start(bf16[24,64,1664]{2,1,0:T(8,128)(2,1)} %all-reduce.25.cloned.1.call-done) | copy-start | bytes 15335428
  425.4 23.6 %copy-start.22 = (f32[24,64]{1,0:T(8,128)}, f32[24,64]{1,0:T(8,128)S(1)}, u32[]{:S(2)}) copy-start(f32[24,64]{1,0:T(8,128)S(1)} %get-tuple-element.14) | copy-start | bytes 18436
  457.4 225.7 %all-reduce.17.cloned.1.call-start = ((), (), s32[]{:S(2)}) async-start(), calls=%async_computation.2 | async-start | bytes 20447232 | tf_op jit(solution)/shard_map/psum | solution.py:87
  481.4 328.9 %all-reduce.29.cloned.1.call-start = ((), (), s32[]{:S(2)}) async-start(), calls=%async_computation.8 | async-start | bytes 10223616 | tf_op jit(solution)/shard_map/psum | solution.py:89
  699.8 16.0 copy-start.3
  699.8 38.2 %copy-start.26 = (f32[24,64]{1,0:T(8,128)}, f32[24,64]{1,0:T(8,128)S(1)}, u32[]{:S(2)}) copy-start(f32[24,64]{1,0:T(8,128)S(1)} %get-tuple-element.12) | copy-start | bytes 18436
  727.0 225.8 %all-reduce.19.cloned.1.call-start = ((), (), s32[]{:S(2)}) async-start(), calls=%async_computation.3 | async-start | bytes 20447232 | tf_op jit(solution)/shard_map/psum | solution.py:92
  758.8 11.9 slice-start.6
  758.8 314.2 %all-reduce.31.cloned.1.call-start = ((), (), s32[]{:S(2)}) async-start(), calls=%async_computation.9 | async-start | bytes 10223616 | tf_op jit(solution)/shard_map/psum | solution.py:94
  758.9 11.8 slice-start.7
  758.9 11.8 slice-start.8
  758.9 11.8 copy-start.15
  770.7 12.4 slice-start.3
  773.2 9.9 slice-start.4
  773.2 9.9 slice-start.5
  791.5 25.2 %copy-start.23 = (f32[24,64]{1,0:T(8,128)S(1)}, f32[24,64]{1,0:T(8,128)}, u32[]{:S(2)}) copy-start(f32[24,64]{1,0:T(8,128)} %copy-done.22) | copy-start | bytes 18436
  791.5 161.3 %copy-start.33 = (f32[24,64]{1,0:T(8,128)S(1)}, f32[24,64]{1,0:T(8,128)}, u32[]{:S(2)}) copy-start(f32[24,64]{1,0:T(8,128)} %copy-done.32) | copy-start | bytes 18436
  969.5 11.8 copy-start.24
  989.8 225.8 %all-reduce.21.cloned.1.call-start = ((), (), s32[]{:S(2)}) async-start(), calls=%async_computation.4 | async-start | bytes 20447232 | tf_op jit(solution)/shard_map/psum | solution.py:87
  1013.7 329.4 %all-reduce.33.cloned.1.call-start = ((), (), s32[]{:S(2)}) async-start(), calls=%async_computation.10 | async-start | bytes 10223616 | tf_op jit(solution)/shard_map/psum | solution.py:89
  1013.7 13.3 copy-start.51
  1013.8 25.3 %slice-start.12 = ((s8[10223616]{0:T(1024)(128)(4,1)}), s8[1835008]{0:T(1024)(128)(4,1)S(1)}, s32[]{:S(2)}) async-start(s8[10223616]{0:T(1024)(128)(4,1)} %bitcast.393), calls=%async_computation.24 | async-start | bytes 3670016
  1027.1 12.0 slice-start.13
  1027.1 12.0 slice-start.14
  1027.1 12.0 copy-start.37
  1027.1 12.0 copy-start.41
  1027.1 12.0 copy-start.46
  1027.1 12.0 copy-start.47
  1045.4 34.1 %copy-start.27 = (f32[24,64]{1,0:T(8,128)S(1)}, f32[24,64]{1,0:T(8,128)}, u32[]{:S(2)}) copy-start(f32[24,64]{1,0:T(8,128)} %copy-done.26) | copy-start | bytes 18436
  1232.5 16.0 copy-start.5
  1232.5 32.8 %copy-start.28 = (f32[24,64]{1,0:T(8,128)}, f32[24,64]{1,0:T(8,128)S(1)}, u32[]{:S(2)}) copy-start(f32[24,64]{1,0:T(8,128)S(1)} %get-tuple-element.8) | copy-start | bytes 18436
  1259.8 225.8 %all-reduce.23.cloned.1.call-start = ((), (), s32[]{:S(2)}) async-start(), calls=%async_computation.5 | async-start | bytes 20447232 | tf_op jit(solution)/shard_map/psum | solution.py:92
  1287.3 320.0 %all-reduce.35.cloned.1.call-start = ((), (), s32[]{:S(2)}) async-start(), calls=%async_computation.11 | async-start | bytes 10223616 | tf_op jit(solution)/shard_map/psum | solution.py:94
  1287.4 28.4 %slice-start.9 = ((s8[10223616]{0:T(1024)(128)(4,1)}), s8[1835008]{0:T(1024)(128)(4,1)S(1)}, s32[]{:S(2)}) async-start(s8[10223616]{0:T(1024)(128)(4,1)} %bitcast.391), calls=%async_computation.21 | async-start | bytes 3670016
  1287.4 28.4 %slice-start.10 = ((s8[10223616]{0:T(1024)(128)(4,1)}), s8[4194304]{0:T(1024)(128)(4,1)S(1)}, s32[]{:S(2)}) async-start(s8[10223616]{0:T(1024)(128)(4,1)} %bitcast.391), calls=%async_computation.22 | async-start | bytes 8388608
  1299.7 16.1 slice-start.11
  1299.7 16.1 copy-start.35
  1299.7 25.5 %slice-start.18 = ((s8[6815744]{0:T(1024)(128)(4,1)}), s8[2621440]{0:T(1024)(128)(4,1)S(1)}, s32[]{:S(2)}) async-start(s8[6815744]{0:T(1024)(128)(4,1)} %bitcast.402), calls=%async_computation.30 | async-start | bytes 5242880
  1299.7 25.5 %slice-start.20 = ((s8[6815744]{0:T(1024)(128)(4,1)}), s8[4194304]{0:T(1024)(128)(4,1)S(1)}, s32[]{:S(2)}) async-start(s8[6815744]{0:T(1024)(128)(4,1)} %bitcast.404), calls=%async_computation.32 | async-start | bytes 8388608
  1335.6 13.9 copy-start.25
  1543.1 70.8 %copy-start.29 = (f32[24,64]{1,0:T(8,128)S(1)}, f32[24,64]{1,0:T(8,128)}, u32[]{:S(2)}) copy-start(f32[24,64]{1,0:T(8,128)} %copy-done.28) | copy-start | bytes 18436
  (41 other events, 210.7 us)
Sparse Core Ops, SparseCore 0:
  40.1 141.0 all-reduce.12
  185.2 83.0 all-reduce.24
  272.5 138.3 all-reduce.14
  457.5 83.0 all-reduce.26
  544.6 138.3 all-reduce.16
  727.1 83.0 all-reduce.28
  814.4 138.3 all-reduce.18
  989.9 83.0 all-reduce.30
  1077.2 138.3 all-reduce.20
  1260.0 83.0 all-reduce.32
  1347.2 138.3 all-reduce.22
  1524.2 83.0 all-reduce.34
where the time goes:
time: 1640 us; the launch traced here: 1630 us
  waiting for transfers between devices  1020 us (62%)
  matrix products  359 us (22%)
  other arithmetic  195 us (12%)
  local copies, waits for them, and re-layouts  25.7 us (2%)
    psum x3, waiting for transfers between devices, device_body(): lower_one = upper_one - lax.psum(f_part, 'tp')  415 us
    psum x3, waiting for transfers between devices, device_body(): lower_two = upper_two - lax.psum(g_part, 'tp')  378 us
    psum x6, waiting for transfers between devices, device_body(): norm_sum = lax.psum(norm_part.astype(jnp.bfloat16), 'tp')  231 us
    reduce_sum x11, other arithmetic, rms_norm(): return x_in * lax.rsqrt(jnp.mean(x_in * x_in, axis=-1, keepdims=True) + EPS)  114 us
    dot_general x3, matrix products, mlp_backward(): jnp.einsum('rsh,fh->rsf', grad_half, w_down, preferred_element_type=jnp.f...  44.2 us
    dot_general x3, matrix products, mlp_backward(): jnp.einsum('rsf,rsh->fh', act_half, grad_half, preferred_element_type=jnp...  37.3 us
    dot_general x3, matrix products, mlp_forward(): jnp.einsum('rsf,fh->rsh', act_half, w_down, preferred_element_type=jnp.fl...  34.5 us
  transfers between devices with their start and end apart: 12, of which 12 were waited for; matrix products, arithmetic and copies ran while one was open for 19% of the time, Pallas kernels for 0%

commit v1 on v0

v1 whole, which is shorter than its diff:
```python
import functools

import jax
import jax.numpy as jnp
from jax import lax
from jax.experimental import pallas as pl
from jax.experimental.pallas import tpu as pltpu
from jax.sharding import PartitionSpec as P

EPS = 1e-6
BF = jnp.bfloat16
F32 = jnp.float32
GROUP = 8
CUT = 896
GELU_K = 0.7978845608028654
MESH = pl.DeviceIdType.MESH
VMEM_LIMIT = 67043328


def rms_norm(x_in):
    return x_in * lax.rsqrt(jnp.mean(x_in * x_in, axis=-1, keepdims=True) + EPS)


def dot(a, b, ca, cb):
    return lax.dot_general(a, b, (((ca,), (cb,)), ((), ())), preferred_element_type=F32)


def tiles(total, size, body):
    def step(i, carry):
        body(pl.multiple_of(i * size, size), size)
        return carry
    lax.fori_loop(0, total // size, step, 0)
    if total % size:
        body(total // size * size, total % size)


def half_block(kind, last, chunks, seq, heads, scale, *refs):
    (n_hbm, g_hbm, w1_hbm, w2_hbm, base_hbm, res_hbm, cot_hbm,
     next_n, next_g, res_out, cot_out, hid_out, dhid_out,
     n_buf, g_buf, w1, w2, own, hid, dhid, aux, s32, k32, r32, x32, y32, s16, k16, r16, x16, y16,
     quad_n, quad_g, qkv, d_att, in_sem, out_sem, send_sem, recv_sem) = refs
    if last:
        quad_n, quad_g = s32, r32
    width = n_buf.shape[-1]
    rows = GROUP * seq
    half = rows // 2
    me = lax.axis_index('tp')
    core, xax, yax = ({'tp': me + bit - 2 * bit * lax.rem(lax.div(me, bit), 2)} for bit in (1, 2, 4))

    barrier = pltpu.get_barrier_semaphore()
    for dev in (core, xax, yax):
        pl.semaphore_signal(barrier, inc=1, device_id=dev, device_id_type=MESH)

    loads = {}

    def load(name, src, dst, i):
        loads[name] = pltpu.make_async_copy(src, dst, in_sem.at[i])
        loads[name].start()

    load('w1', w1_hbm, w1, 0)
    for k in range(chunks):
        load(('n', k), n_hbm.at[pl.ds(k * rows, rows)], n_buf.at[k], 2 + 5 * k)
        if k == 0:
            load('w2', w2_hbm, w2, 1)
        load(('g', k), g_hbm.at[pl.ds(k * rows, rows)], g_buf.at[k], 3 + 5 * k)
    for k in range(chunks):
        for j, src in enumerate((base_hbm, res_hbm, cot_hbm)):
            load(('own', j, k), src.at[k], own.at[j, k], 4 + 5 * k + j)
    pl.semaphore_wait(barrier, 3)

    sent = []
    saved = []
    done = set()

    def remote(k, i, src, dst, dev):
        copy = pltpu.make_async_remote_copy(src_ref=src, dst_ref=dst, send_sem=send_sem.at[k, i],
                                            recv_sem=recv_sem.at[k, i], device_id=dev, device_id_type=MESH)
        copy.start()
        sent.append(copy)
        return copy

    def save(k, i, src, dst):
        copy = pltpu.make_async_copy(src, dst, out_sem.at[k, i])
        copy.start()
        saved.append(copy)
        return copy

    cols_a, cols_b = pl.ds(0, CUT), pl.ds(CUT, width - CUT)
    flight = {}
    slot_free = {}

    def blocks(v):
        return v.reshape(2, 2, seq, v.shape[-1])

    def send_partial(k, lhs, w, cw, s_ref, k_ref, name, i):
        def make(out, part):
            def tile(off, size):
                a = lhs[part * half:(part + 1) * half, :]
                b = w[:, pl.ds(off, size)] if cw == 0 else w[pl.ds(off, size), :]
                out[k, :, :, :, pl.ds(off, size)] = blocks(dot(a, b, 1, cw).astype(out.dtype))
            tiles(width, 256, tile)
        make(s_ref, 1)
        recv = r32 if name == 'f' else r16
        flight[name, k] = [remote(k, i, s_ref.at[k], recv.at[k], core)]
        make(k_ref, 0)

    def forward(k):
        slot = k % 2
        if k == 0:
            loads['w1'].wait()
        loads['n', k].wait()
        if k >= 2:
            for copy in slot_free[k - 2]:
                copy.wait()
                done.add(id(copy))
        if kind == 'mlp':
            def tile(off, size):
                u = dot(n_buf[k], w1[:, pl.ds(off, size)], 1, 0)
                t = jnp.tanh(GELU_K * (u + 0.044715 * u * u * u))
                hid[slot, :, pl.ds(off, size)] = (0.5 * u * (1.0 + t)).astype(BF)
                aux[:, pl.ds(off, size)] = 0.5 * (1.0 + t) + 0.5 * u * (1.0 - t * t) * (
                    GELU_K * (1.0 + 3 * 0.044715 * u * u))
            tiles(hid.shape[-1], 256, tile)
        else:
            def tile(off, size):
                qkv[:, pl.ds(off, size)] = dot(n_buf[k], w1[:, pl.ds(off, size)], 1, 0).astype(BF)
            tiles(qkv.shape[-1], 256, tile)
            dim = qkv.shape[-1] // (3 * heads)

            def one_seq(s, carry):
                r = pl.ds(pl.multiple_of(s * seq, seq), seq)
                for h in range(heads):
                    q = qkv[r, h * dim:(h + 1) * dim]
                    key = qkv[r, (heads + h) * dim:(heads + h + 1) * dim]
                    v = qkv[r, (2 * heads + h) * dim:(2 * heads + h + 1) * dim]
                    scores = dot(q, key, 1, 1) * scale
                    expd = jnp.exp(scores - jnp.max(scores, axis=-1, keepdims=True))
                    prob = expd / jnp.sum(expd, axis=-1, keepdims=True)
                    aux[r, h * seq:(h + 1) * seq] = prob
                    hid[slot, r, h * dim:(h + 1) * dim] = dot(prob.astype(BF), v, 1, 0).astype(BF)
                return carry
            lax.fori_loop(0, GROUP, one_seq, 0, unroll=4)
        first = save(k, 0, hid.at[slot], hid_out.at[pl.ds(k * rows, rows)])
        slot_free[k] = [first]
        if k == 0:
            loads['w2'].wait()
        send_partial(k, hid.at[slot], w2, 0, s32, k32, 'f', 0)

    def backward(k):
        slot = k % 2
        loads['g', k].wait()
        if kind == 'mlp':
            def tile(off, size):
                d_act = dot(g_buf[k], w2[pl.ds(off, size), :], 1, 1)
                dhid[slot, :, pl.ds(off, size)] = (d_act * aux[:, pl.ds(off, size)]).astype(BF)
            tiles(dhid.shape[-1], 256, tile)
        else:
            dim = qkv.shape[-1] // (3 * heads)
            d_att[...] = dot(g_buf[k], w2[...], 1, 1).astype(BF)

            def one_seq(s, carry):
                r = pl.ds(pl.multiple_of(s * seq, seq), seq)
                for h in range(heads):
                    q = qkv[r, h * dim:(h + 1) * dim]
                    key = qkv[r, (heads + h) * dim:(heads + h + 1) * dim]
                    v = qkv[r, (2 * heads + h) * dim:(2 * heads + h + 1) * dim]
                    prob = aux[r, h * seq:(h + 1) * seq]
                    d_out = d_att[r, h * dim:(h + 1) * dim]
                    d_prob = dot(d_out, v, 1, 1).astype(BF).astype(F32)
                    row_dot = jnp.sum(d_prob * prob, axis=-1, keepdims=True)
                    d_score = (prob * (d_prob - row_dot) * scale).astype(BF)
                    dhid[slot, r, h * dim:(h + 1) * dim] = dot(d_score, key, 1, 0).astype(BF)
                    dhid[slot, r, (heads + h) * dim:(heads + h + 1) * dim] = dot(d_score, q, 0, 0).astype(BF)
                    dhid[slot, r, (2 * heads + h) * dim:(2 * heads + h + 1) * dim] = dot(
                        prob.astype(BF), d_out, 0, 0).astype(BF)
                return carry
            lax.fori_loop(0, GROUP, one_seq, 0, unroll=4)
        slot_free[k].append(save(k, 1, dhid.at[slot], dhid_out.at[pl.ds(k * rows, rows)]))
        send_partial(k, dhid.at[slot], w1, 1, s16, k16, 'n', 5)

    bufs = {'f': (k32, r32, x32, y32, 0), 'n': (k16, r16, x16, y16, 5)}

    def core_done(name, k):
        kb, rb, xb, yb, i = bufs[name]
        flight[name, k][0].wait_recv()
        if last:
            flight[name, k][0].wait_send()
            done.add(id(flight[name, k][0]))
        dt = kb.dtype
        for bx in (1, 0):
            for by in (1, 0):
                kb[k, bx, by] = (kb[k, bx, by].astype(F32) + rb[k, bx, by].astype(F32)).astype(dt)
        flight[name, k] = [remote(k, i + 1, kb.at[k, 1, :, :, cols_a], xb.at[k, :, :, cols_a], xax),
                           remote(k, i + 2, kb.at[k, :, 1, :, cols_b], xb.at[k, :, :, cols_b], yax)]

    def second_done(name, k):
        kb, rb, xb, yb, i = bufs[name]
        dt = kb.dtype
        copy_a, copy_b = flight[name, k]
        copy_a.wait_recv()
        for j in (1, 0):
            kb[k, 0, j, :, :CUT] = (kb[k, 0, j, :, :CUT].astype(F32) + xb[k, j, :, :CUT].astype(F32)).astype(dt)
        third_a = remote(k, i + 3, kb.at[k, 0, 1, :, cols_a], yb.at[k, :, cols_a], yax)
        copy_b.wait_recv()
        for j in (1, 0):
            kb[k, j, 0, :, CUT:] = (kb[k, j, 0, :, CUT:].astype(F32) + xb[k, j, :, CUT:].astype(F32)).astype(dt)
        third_b = remote(k, i + 4, kb.at[k, 1, 0, :, cols_b], yb.at[k, :, cols_b], xax)
        flight[name, k] = [third_a, third_b]

    def gather_start(name, k, quad, i):
        flight[name, k] = [
            remote(k, i, quad.at[k, 0, 0, :, cols_a], quad.at[k, 0, 1, :, cols_a], yax),
            remote(k, i + 1, quad.at[k, 0, 0, :, cols_b], quad.at[k, 1, 0, :, cols_b], xax)]

    def third_done(name, k):
        kb, rb, xb, yb, i = bufs[name]
        for copy in flight[name, k]:
            copy.wait_recv()
        summed = kb[k, 0, 0].astype(F32) + yb[k].astype(F32)
        if name == 'f':
            loads['own', 1, k].wait()
            value = own[1, k] - summed
            own[1, k] = value
            save(k, 2, own.at[1, k], res_out.at[k])
            quad_n[k, 0, 0] = value if last else rms_norm(value).astype(BF)
            gather_start('gn', k, quad_n, 10)
        else:
            loads['own', 0, k].wait()
            loads['own', 2, k].wait()
            x_in = own[0, k]
            inv = lax.rsqrt(jnp.mean(x_in * x_in, axis=-1, keepdims=True) + EPS)
            proj = jnp.mean(x_in * summed, axis=-1, keepdims=True)
            value = own[2, k] + (inv * summed - x_in * (inv * inv * inv * proj))
            own[2, k] = value
            save(k, 3, own.at[2, k], cot_out.at[k])
            quad_g[k, 0, 0] = value.astype(quad_g.dtype)
            gather_start('gg', k, quad_g, 15)

    def gather_second(name, k):
        quad, i = (quad_n, 10) if name == 'gn' else (quad_g, 15)
        copy_a, copy_b = flight[name, k]
        copy_a.wait_recv()
        second_a = remote(k, i + 2, quad.at[k, 0, :, :, cols_a], quad.at[k, 1, :, :, cols_a], xax)
        copy_b.wait_recv()
        second_b = remote(k, i + 3, quad.at[k, :, 0, :, cols_b], quad.at[k, :, 1, :, cols_b], yax)
        flight[name, k] = [second_a, second_b]

    arrivals = []

    def gather_core(name, k):
        quad, i, out = (quad_n, 10, next_n) if name == 'gn' else (quad_g, 15, next_g)
        for copy in flight[name, k]:
            copy.wait_recv()
        arrivals.append(remote(k, i + 4, quad.at[k], out.at[k, 1], core))
        save(k, 4 if name == 'gn' else 5, quad.at[k], out.at[k, 0])

    def compute(k):
        forward(k)
        backward(k)
        core_done('f', k)
        core_done('n', k)

    def stage(fn, k, a='f', b='n'):
        fn(a, k)
        fn(b, k)

    lags = [compute, lambda k: stage(second_done, k), lambda k: stage(third_done, k),
            lambda k: stage(gather_second, k, 'gn', 'gg'), lambda k: stage(gather_core, k, 'gn', 'gg')]
    for step in range(chunks + len(lags) - 1):
        for j, fn in enumerate(lags):
            k = step - j
            if 0 <= k < chunks:
                fn(k)

    for copy in arrivals:
        copy.wait_recv()
    for copy in sent:
        if id(copy) not in done:
            copy.wait_send()
    for copy in saved:
        if id(copy) not in done:
            copy.wait()


def run_half(kind, last, ident, n, g, w1, w2, base, res, cot, heads, scale):
    chunks, seq, width = base.shape
    rows = GROUP * seq
    hid = w2.shape[0]
    dhid = w1.shape[1]
    wide = F32 if last else BF
    total = chunks * rows
    gathered = jax.ShapeDtypeStruct((chunks, 2, 2, 2, seq, width), wide)
    own = jax.ShapeDtypeStruct((chunks, seq, width), F32)
    quad = (chunks, 2, 2, seq, width)
    small = (8, 128)
    mlp = kind == 'mlp'
    scratch = [pltpu.VMEM((chunks, rows, width), BF), pltpu.VMEM((chunks, rows, width), BF),
               pltpu.VMEM(w1.shape, BF), pltpu.VMEM(w2.shape, BF),
               pltpu.VMEM((3, chunks, seq, width), F32),
               pltpu.VMEM((2, rows, hid), BF), pltpu.VMEM((2, rows, dhid), BF),
               pltpu.VMEM((rows, hid if mlp else heads * seq), F32)]
    for dt in (F32, BF):
        scratch += [pltpu.VMEM(quad, dt)] * 3
        scratch += [pltpu.VMEM((chunks, 2, seq, width), dt), pltpu.VMEM((chunks, seq, width), dt)]
    scratch += [pltpu.VMEM(small if last else quad, BF)] * 2
    scratch += [pltpu.VMEM(small if mlp else (rows, dhid), BF), pltpu.VMEM(small if mlp else (rows, hid), BF)]
    scratch += [pltpu.SemaphoreType.DMA((2 + 5 * chunks,)), pltpu.SemaphoreType.DMA((chunks, 6)),
                pltpu.SemaphoreType.DMA((chunks, 20)), pltpu.SemaphoreType.DMA((chunks, 20))]
    any_spec = pl.BlockSpec(memory_space=pl.ANY)
    flops = 6 * total * width * (hid + dhid)
    return pl.pallas_call(
        functools.partial(half_block, kind, last, chunks, seq, heads, scale),
        out_shape=[gathered, gathered, own, own,
                   jax.ShapeDtypeStruct((total, hid), BF), jax.ShapeDtypeStruct((total, dhid), BF)],
        in_specs=[any_spec] * 7,
        out_specs=[any_spec] * 6,
        scratch_shapes=scratch,
        compiler_params=pltpu.CompilerParams(collective_id=ident, has_side_effects=True, vmem_limit_bytes=VMEM_LIMIT),
        cost_estimate=pl.CostEstimate(flops=flops, bytes_accessed=total * width * 12, transcendentals=total * hid),
        name=kind + ('_last' if last else ''),
    )(n, g, w1, w2, base, res, cot)


def order_blocks(blocks, me_bits):
    return jnp.concatenate([lax.dynamic_slice_in_dim(blocks, p ^ me_bits, 1, axis=1) for p in range(GROUP)], axis=1)


def solution(mesh):
    act_spec = P('dp')
    in_specs = (act_spec, act_spec, act_spec, act_spec,
                P(None, None, None, 'tp', None), P(None, 'tp', None, None),
                P(None, None, 'tp'), P(None, 'tp', None))
    out_specs = (act_spec, act_spec, act_spec, act_spec,
                 P('dp', None, None, 'tp', None), P('dp', 'tp', None, None),
                 P('dp', None, 'tp'), P('dp', 'tp', None))

    def device_body(y_one, y_two, dy_one, dy_two, w_qkv, w_out, w_up, w_down):
        n_micro, n_batch, seq, width = y_one.shape
        layers, heads, head_dim = w_qkv.shape[0], w_qkv.shape[3], w_qkv.shape[4]
        scale = head_dim ** -0.5
        pad = -head_dim % 128
        pdim = head_dim + pad
        chunks = n_micro * n_batch // GROUP
        total = chunks * GROUP * seq
        index = lax.axis_index('tp')
        me_bits = (index & 1) * 4 + (index & 2) + (index >> 2)

        full = [a.reshape(chunks, GROUP, seq, width) for a in (y_one, y_two, dy_one, dy_two)]
        one, two, g_one, g_two = [lax.dynamic_slice_in_dim(a, me_bits, 1, axis=1)[:, 0] for a in full]
        normed = order_blocks(rms_norm(full[0]).astype(BF), me_bits).reshape(total, width)
        grads = order_blocks(full[3].astype(BF), me_bits).reshape(total, width)

        w_qkv_p = jnp.pad(w_qkv, ((0, 0),) * 4 + ((0, pad),)).reshape(layers, width, 3 * heads * pdim)
        w_out_p = jnp.pad(w_out, ((0, 0), (0, 0), (0, pad), (0, 0))).reshape(layers, heads * pdim, width)

        d_qkv, d_out, d_up, d_down = [], [], [], []
        for layer in reversed(range(layers)):
            last = layer == 0
            nn, ng, two, g_one, act, d_pre = run_half(
                'mlp', last, 2 * last, normed, grads, w_up[layer], w_down[layer], one, two, g_one, heads, scale)
            d_down.append(dot(act, grads, 0, 0))
            d_up.append(dot(normed, d_pre, 0, 0))
            if last:
                nn, ng = (v.reshape(chunks, GROUP, seq, width) for v in (nn, ng))
                out_two, out_g_one = order_blocks(nn, me_bits), order_blocks(ng, me_bits)
                nn, ng = rms_norm(nn).astype(BF), ng.astype(BF)
            normed, grads = nn.reshape(total, width), ng.reshape(total, width)
            nn, ng, one, g_two, att, d_proj = run_half(
                'attn', last, 1 + 2 * last, normed, grads, w_qkv_p[layer], w_out_p[layer], two, one, g_two, heads, scale)
            d_out.append(dot(att, grads, 0, 0).reshape(heads, pdim, width)[:, :head_dim])
            d_qkv.append(dot(normed, d_proj, 0, 0).reshape(width, 3, heads, pdim)[..., :head_dim])
            if last:
                nn, ng = (v.reshape(chunks, GROUP, seq, width) for v in (nn, ng))
                out_one, out_g_two = order_blocks(nn, me_bits), order_blocks(ng, me_bits)
            normed, grads = nn.reshape(total, width), ng.reshape(total, width)

        acts = [v.reshape(y_one.shape) for v in (out_one, out_two, out_g_one, out_g_two)]
        return (*acts, jnp.stack(d_qkv[::-1]), jnp.stack(d_out[::-1]), jnp.stack(d_up[::-1]), jnp.stack(d_down[::-1]))

    return jax.shard_map(device_body, mesh=mesh, in_specs=in_specs, out_specs=out_specs, check_vma=False)
```

time: 1640 us -> 1150 us (0.70)
  waiting for transfers between devices: 1020 us -> 0 us
  Pallas kernels: 0 us -> 895 us
  matrix products: 359 us -> 97 us
  other arithmetic: 195 us -> 60.4 us
  local copies, waits for them, and re-layouts: 25.7 us -> 89.3 us
    psum x12 -> x0, waiting for transfers between devices: 1020 us -> none  [the longest x3 415 us: device_body(): lower_one = upper_one - lax.psum(f_part, 'tp')]
    pallas_call x0 -> x6, Pallas kernels: none -> 895 us  [run_half(): pl.pallas_call(functools.partial(half_block, kind, last, chunks, seq, hea...]
    dot_general x51 -> x12, matrix products: 349 us -> 97 us  [dot(): lax.dot_general(a, b, (((ca,), (cb,)), ((), ())), preferred_element_type=...]
    reduce_sum x11 -> x2, other arithmetic: 114 us -> 9.44 us  [rms_norm(): return x_in * lax.rsqrt(jnp.mean(x_in * x_in, axis=-1, keepdims=True) + EPS)]
    add x4 -> x0, other arithmetic: 34.2 us -> none  [the longest x2 22.2 us: device_body(): grad_one = grad_one + norm_back(upper_one, norm_sum.astype(jnp.float32))]
    squeeze x0 -> x9, local copies, waits for them, and re-layouts: none -> 33.8 us  [the longest x3 12 us: device_body(): w_qkv_p[layer]]
    unnamed x154 -> x120, local copies, waits for them, and re-layouts: 25.7 us -> 34.8 us
  transfers between devices with their start and end apart: 12 -> 0, of which waited for: 12 -> 0; matrix products, arithmetic and copies ran while one was open for 19% -> 0% of each run, Pallas kernels for 0% -> 0%
where the time goes in v1:
time: 1150 us; the launch traced here: 1140 us
  Pallas kernels  895 us (78%)
  matrix products  97 us (8%)
  local copies, waits for them, and re-layouts  89.3 us (8%)
  other arithmetic  60.4 us (5%)
    pallas_call x6, Pallas kernels, run_half(): pl.pallas_call(functools.partial(half_block, kind, last, chunks, seq, hea...  895 us
    dot_general x12, matrix products, dot(): lax.dot_general(a, b, (((ca,), (cb,)), ((), ())), preferred_element_type=...  97 us
    unnamed x120, local copies, waits for them, and re-layouts  34.8 us

profile of v1, /device:TPU:0, one launch (start us, length us, event | category | flops | bytes accessed | tf_op | source)
XLA Modules:
  0.0 1143.0 jit_solution(8535517427998815551)
XLA Ops:
  0.7 4.6 multiply_reduce_fusion.1
  5.4 2.6 dynamic-slice_bitcast_fusion.3.refs_4_.refs_5_
  8.0 2.5 dynamic-slice_bitcast_fusion.2.refs_5_
  10.4 2.4 dynamic-slice_bitcast_fusion.1.refs_6_
  12.9 2.4 dynamic-slice_bitcast_fusion.refs_6_
  15.3 1.6 pad_slice_fusion.3
  16.9 4.5 multiply_convert_fusion.1
  21.5 4.5 convert_element_type.28
  27.4 1.9 copy-done.9
  29.3 2.6 copy-done.10
  33.0 3.2 pad_slice_fusion
  36.2 4.5 copy.47.refs_2_
  40.7 2.9 copy.46.refs_2_
  43.6 4.5 copy.45.refs_2_
  48.1 7.8 slice_bitcast_fusion.1
  58.1 4.0 slice_bitcast_fusion
  62.1 131.3 %mlp.2 = (bf16[3,2,2,2,64,1664]{5,4,3,2,1,0:T(8,128)(2,1)}, bf16[3,2,2,2,64,1664]{5,4,3,2,1,0:T(8,128)(2,1)}, f32[3,64,1664]{2,1,0:T(8,128)}, f32[3,64,1664]{2,1...) custom-call(bf16[1536,1664]{1,0:T(8,128)(2,1)} %bitcast.222, bf16[1536,1664]{1,0:T(8,128)(2,1)} %bitcast.220, ...), custom_call_target="tpu_custom_call" | custom-call | flops 31406948352 | bytes 30670848 | tf_op jit(solution)/shard_map/mlp/pallas_call | solution.py:311
  193.4 10.6 convolution_bitcast_fusion.3
  204.0 10.4 convolution_bitcast_fusion
  214.4 138.2 %attn.2 = (bf16[3,2,2,2,64,1664]{5,4,3,2,1,0:T(8,128)(2,1)}, bf16[3,2,2,2,64,1664]{5,4,3,2,1,0:T(8,128)(2,1)}, f32[3,64,1664]{2,1,0:T(8,128)}, f32[3,64,1664]{2,...) custom-call(bf16[1536,1664]{1,0:T(8,128)(2,1)} %bitcast.228, bf16[1536,1664]{1,0:T(8,128)(2,1)} %bitcast.196, ...), custom_call_target="tpu_custom_call" | custom-call | flops 15703474176 | bytes 30670848 | tf_op jit(solution)/shard_map/attn/pallas_call | solution.py:311
  354.2 4.9 convolution_bitcast_fusion.9
  359.1 2.8 copy.50
  361.9 8.7 convolution_bitcast_fusion.6
  370.6 131.0 %mlp.3 = (bf16[3,2,2,2,64,1664]{5,4,3,2,1,0:T(8,128)(2,1)}, bf16[3,2,2,2,64,1664]{5,4,3,2,1,0:T(8,128)(2,1)}, f32[3,64,1664]{2,1,0:T(8,128)}, f32[3,64,1664]{2,1...) custom-call(bf16[1536,1664]{1,0:T(8,128)(2,1)} %bitcast.234, bf16[1536,1664]{1,0:T(8,128)(2,1)} %bitcast.230, ...), custom_call_target="tpu_custom_call" | custom-call | flops 31406948352 | bytes 30670848 | tf_op jit(solution)/shard_map/mlp/pallas_call | solution.py:311
  501.6 10.6 convolution_bitcast_fusion.4
  512.1 10.4 convolution_bitcast_fusion.1
  522.5 138.2 %attn.3 = (bf16[3,2,2,2,64,1664]{5,4,3,2,1,0:T(8,128)(2,1)}, bf16[3,2,2,2,64,1664]{5,4,3,2,1,0:T(8,128)(2,1)}, f32[3,64,1664]{2,1,0:T(8,128)}, f32[3,64,1664]{2,...) custom-call(bf16[1536,1664]{1,0:T(8,128)(2,1)} %bitcast.232, bf16[1536,1664]{1,0:T(8,128)(2,1)} %bitcast.198, ...), custom_call_target="tpu_custom_call" | custom-call | flops 15703474176 | bytes 30670848 | tf_op jit(solution)/shard_map/attn/pallas_call | solution.py:311
  662.3 4.9 convolution_bitcast_fusion.10
  667.2 2.8 copy.49
  670.0 8.6 convolution_bitcast_fusion.7
  678.6 174.3 %mlp_last.1 = (f32[3,2,2,2,64,1664]{5,4,3,2,1,0:T(8,128)}, f32[3,2,2,2,64,1664]{5,4,3,2,1,0:T(8,128)}, f32[3,64,1664]{2,1,0:T(8,128)}, f32[3,64,1664]{2,1,0:T(8,...) custom-call(bf16[1536,1664]{1,0:T(8,128)(2,1)} %bitcast.226, bf16[1536,1664]{1,0:T(8,128)(2,1)} %bitcast.224, ...), custom_call_target="tpu_custom_call" | custom-call | flops 31406948352 | bytes 30670848 | tf_op jit(solution)/shard_map/mlp_last/pallas_call | solution.py:311
  852.9 4.8 multiply_reduce_fusion
  857.8 9.1 convolution_bitcast_fusion.5
  867.0 12.9 %pad_maximum_fusion = f32[3,1664,1024]{2,1,0:T(8,128)} fusion(f32[1,1664,1024]{2,1,0:T(8,128)S(1)} %bitcast.190, f32[1,1664,1024]{2,1,0:T(8,128)} %convolution_bitcast_fusion.4, f32[1,1664,1024]{2,1,0:T(8,128)S(1)} %convolution_bitcast_fusion.5), kind=kLoop, calls=%fused_computation | loop fusion | flops 10223616 | bytes 40894464 | tf_op jit(solution)/shard_map/stack | solution.py:378
  879.9 8.6 convolution_bitcast_fusion.2
  888.6 7.4 pad_maximum_fusion.1
  896.0 2.9 multiply_convert_fusion
  899.0 3.0 fusion.refs_0_
  901.9 6.9 convert_element_type.30
  908.8 181.8 %attn_last.1 = (f32[3,2,2,2,64,1664]{5,4,3,2,1,0:T(8,128)}, f32[3,2,2,2,64,1664]{5,4,3,2,1,0:T(8,128)}, f32[3,64,1664]{2,1,0:T(8,128)}, f32[3,64,1664]{2,1,0:T(8...) custom-call(bf16[1536,1664]{1,0:T(8,128)(2,1)} %fusion.refs_0_, bf16[1536,1664]{1,0:T(8,128)(2,1)} %bitcast.158, ...), custom_call_target="tpu_custom_call" | custom-call | flops 15703474176 | bytes 30670848 | tf_op jit(solution)/shard_map/attn_last/pallas_call | solution.py:311
  1092.1 3.8 convolution_bitcast_fusion.11
  1095.9 2.3 pad_maximum_fusion.3
  1098.2 3.0 copy.48
  1101.3 6.5 convolution_bitcast_fusion.8
  1107.9 6.5 pad_maximum_fusion.2
  1116.6 1.6 dynamic-slice_dynamic-update-slice_fusion.7
  1135.7 3.8 copy-done.7
  1139.5 3.4 copy-done.8
  (138 shorter events, 28.9 us)
Async XLA Ops:
  5.3 10.0 copy-start.6
  26.4 5.5 slice-start.24
  26.7 2.6 copy-start.9
  26.9 6.1 slice-start.25
  29.3 2.6 copy-start.10
  43.6 12.4 %slice-start.9 = ((s8[10223616]{0:T(1024)(128)(4,1)}), s8[1835008]{0:T(1024)(128)(4,1)S(1)}, s32[]{:S(2)}) async-start(s8[10223616]{0:T(1024)(128)(4,1)} %bitcast.162), calls=%async_computation.9 | async-start | bytes 3670016
  48.1 8.7 slice-start.10
  48.1 10.0 slice-start.11
  193.4 10.6 copy-start.12
  352.6 6.5 copy-start.4
  501.6 10.6 copy-start.13
  660.7 6.4 copy-start.5
  852.9 14.0 %slice-start.20 = ((s8[6815744]{0:T(1024)(128)(4,1)}), s8[2621440]{0:T(1024)(128)(4,1)S(1)}, s32[]{:S(2)}) async-start(s8[6815744]{0:T(1024)(128)(4,1)} %bitcast.189), calls=%async_computation.20 | async-start | bytes 5242880
  857.8 9.1 slice-start.21
  857.8 30.7 %slice-start.18 = ((s8[6815744]{0:T(1024)(128)(4,1)}), s8[4194304]{0:T(1024)(128)(4,1)S(1)}, s32[]{:S(2)}) async-start(s8[6815744]{0:T(1024)(128)(4,1)} %bitcast.187), calls=%async_computation.18 | async-start | bytes 8388608
  857.8 30.7 %slice-start.22 = ((s8[6815744]{0:T(1024)(128)(4,1)}), s8[4194304]{0:T(1024)(128)(4,1)S(1)}, s32[]{:S(2)}) async-start(s8[6815744]{0:T(1024)(128)(4,1)} %bitcast.191), calls=%async_computation.22 | async-start | bytes 8388608
  867.0 12.9 %copy-start.11 = (bf16[1536,1024]{1,0:T(8,128)(2,1)S(1)}, bf16[1536,1024]{1,0:T(8,128)(2,1)}, u32[]{:S(2)}) copy-start(bf16[1536,1024]{1,0:T(8,128)(2,1)} %get-tuple-element.71) | copy-start | bytes 9437188
  867.0 21.6 %slice-start.19 = ((s8[6815744]{0:T(1024)(128)(4,1)}), s8[2621440]{0:T(1024)(128)(4,1)S(1)}, s32[]{:S(2)}) async-start(s8[6815744]{0:T(1024)(128)(4,1)} %bitcast.187), calls=%async_computation.19 | async-start | bytes 5242880
  867.0 21.5 %slice-start.23 = ((s8[6815744]{0:T(1024)(128)(4,1)}), s8[2621440]{0:T(1024)(128)(4,1)S(1)}, s32[]{:S(2)}) async-start(s8[6815744]{0:T(1024)(128)(4,1)} %bitcast.191), calls=%async_computation.23 | async-start | bytes 5242880
  879.9 16.1 %slice-start = ((s8[10223616]{0:T(1024)(128)(4,1)}), s8[4194304]{0:T(1024)(128)(4,1)S(1)}, s32[]{:S(2)}) async-start(s8[10223616]{0:T(1024)(128)(4,1)} %bitcast.134), calls=%async_computation | async-start | bytes 8388608
  879.9 16.1 %slice-start.1 = ((s8[10223616]{0:T(1024)(128)(4,1)}), s8[4194304]{0:T(1024)(128)(4,1)S(1)}, s32[]{:S(2)}) async-start(s8[10223616]{0:T(1024)(128)(4,1)} %bitcast.134), calls=%async_computation.1 | async-start | bytes 8388608
  888.6 7.4 slice-start.2
  1090.5 5.4 copy-start
  1090.6 5.4 copy-start.1
  1101.2 6.6 copy-start.2
  1101.2 6.6 copy-start.3
  1101.2 13.1 %slice-start.6 = ((s8[10223616]{0:T(1024)(128)(4,1)}), s8[4194304]{0:T(1024)(128)(4,1)S(1)}, s32[]{:S(2)}) async-start(s8[10223616]{0:T(1024)(128)(4,1)} %bitcast.148), calls=%async_computation.6 | async-start | bytes 8388608
  1101.2 13.1 %slice-start.7 = ((s8[10223616]{0:T(1024)(128)(4,1)}), s8[4194304]{0:T(1024)(128)(4,1)S(1)}, s32[]{:S(2)}) async-start(s8[10223616]{0:T(1024)(128)(4,1)} %bitcast.148), calls=%async_computation.7 | async-start | bytes 8388608
  1101.2 13.1 %slice-start.15 = ((s8[10223616]{0:T(1024)(128)(4,1)}), s8[4194304]{0:T(1024)(128)(4,1)S(1)}, s32[]{:S(2)}) async-start(s8[10223616]{0:T(1024)(128)(4,1)} %bitcast.174), calls=%async_computation.15 | async-start | bytes 8388608
  1101.3 14.0 %slice-start.16 = ((s8[10223616]{0:T(1024)(128)(4,1)}), s8[4194304]{0:T(1024)(128)(4,1)S(1)}, s32[]{:S(2)}) async-start(s8[10223616]{0:T(1024)(128)(4,1)} %bitcast.174), calls=%async_computation.16 | async-start | bytes 8388608
  1107.8 8.2 slice-start.8
  1107.8 8.7 slice-start.17
  1118.2 15.8 %slice-start.12 = ((s8[10223616]{0:T(1024)(128)(4,1)}), s8[4194304]{0:T(1024)(128)(4,1)S(1)}, s32[]{:S(2)}) async-start(s8[10223616]{0:T(1024)(128)(4,1)} %bitcast.164), calls=%async_computation.12 | async-start | bytes 8388608
  1122.7 11.3 slice-start.13
  1125.0 9.0 slice-start.3
  1127.2 6.8 slice-start.4
  1128.4 5.7 slice-start.14
  1130.6 3.4 slice-start.5
  1135.5 4.0 copy-start.7
  1135.7 7.2 copy-start.8

commit v2 on v0

v2 whole, which is shorter than its diff:
```python
import functools

import jax
import jax.numpy as jnp
from jax import lax
from jax.experimental import pallas as pl
from jax.experimental.pallas import tpu as pltpu
from jax.sharding import PartitionSpec as P

EPS = 1e-6
BF = jnp.bfloat16
F32 = jnp.float32
GROUP = 8
CUT = 896
GELU_K = 0.7978845608028654
MESH = pl.DeviceIdType.MESH
VMEM_LIMIT = 67043328


def rms_norm(x_in):
    return x_in * lax.rsqrt(jnp.mean(x_in * x_in, axis=-1, keepdims=True) + EPS)


def dot(a, b, ca, cb):
    return lax.dot_general(a, b, (((ca,), (cb,)), ((), ())), preferred_element_type=F32)


def tiles(total, size, body):
    def step(i, carry):
        body(pl.multiple_of(i * size, size), size)
        return carry
    lax.fori_loop(0, total // size, step, 0)
    if total % size:
        body(total // size * size, total % size)


def backward_pass(layers, chunks, seq, heads, dim, scale, *refs):
    (y1, y2, dy1, dy2, wa_hbm, wu_hbm, wd_hbm,
     x1, x2, dx1, dx2, dwa, dwu, dwd, next_n, next_g,
     n_buf, g_buf, w1, w2, own, hid, dhid, aux, s32, k32, r32, x32, y32, s16, k16, r16, x16, y16,
     quad_n, quad_g, in_sem, first_sem, own_sem, w_sem, wg_sem, out_sem, send_sem, recv_sem, fsend_sem, frecv_sem) = refs
    width = n_buf.shape[-1]
    rows = GROUP * seq
    half = rows // 2
    att_w = heads * dim
    me = lax.axis_index('tp')
    my_core, my_x, my_y = lax.rem(me, 2), lax.rem(lax.div(me, 2), 2), lax.rem(lax.div(me, 4), 2)
    core, xax, yax = {'tp': me + 1 - 2 * my_core}, {'tp': me + 2 - 4 * my_x}, {'tp': me + 4 - 8 * my_y}

    barrier = pltpu.get_barrier_semaphore()
    for dev in (core, xax, yax):
        pl.semaphore_signal(barrier, inc=1, device_id=dev, device_id_type=MESH)

    def local(src, dst, sem):
        copy = pltpu.make_async_copy(src, dst, sem)
        copy.start()
        return copy

    loads = {}

    def load_weights(h):
        layer = layers - 1 - h // 2
        if h % 2 == 0:
            loads['w1'] = local(wu_hbm.at[layer], w1, w_sem.at[0])
            loads['w2'] = local(wd_hbm.at[layer], w2, w_sem.at[1])
        else:
            loads['w2'] = local(wa_hbm.at[layer], w2, w_sem.at[1])

    def place(k, c, bx, by):
        return k * GROUP + 4 * (my_core + c - 2 * c * my_core) + 2 * (my_x + bx - 2 * bx * my_x) + (
            my_y + by - 2 * by * my_y)

    firsts = [(k, src) for k in range(chunks) for src in (0, 1)]

    def fetch_first(i):
        k, src = firsts[i]
        slot = 1 + src
        loads['first', i] = [
            local((dy2 if src else y1).at[place(k, c, b // 2, b % 2)], (k32 if c else s32).at[slot, b // 2, b % 2],
                  first_sem.at[src, 4 * c + b]) for c in range(2) for b in range(4)]

    def round_first(i):
        k, src = firsts[i]
        slot = 1 + src
        for copy in loads.pop(('first', i)):
            copy.wait()
        for c in range(2):
            def one(b, carry):
                value = (k32 if c else s32)[slot, lax.div(b, 2), lax.rem(b, 2)]
                if src == 0:
                    n_buf[k, c, lax.div(b, 2), lax.rem(b, 2)] = rms_norm(value).astype(BF)
                else:
                    g_buf[k, c, lax.div(b, 2), lax.rem(b, 2)] = value.astype(BF)
                return carry
            lax.fori_loop(0, 4, one, 0)
        if i + 2 < len(firsts):
            fetch_first(i + 2)

    fetch_first(0)
    load_weights(0)
    fetch_first(1)
    mine = place(0, 0, 0, 0)
    for k in range(chunks):
        for j, src in enumerate((y1, y2, dy1, dy2)):
            loads['own', j, k] = local(src.at[k * GROUP + mine], own.at[j, k], own_sem.at[k, j])
    pl.semaphore_wait(barrier, 3)
    round_first(0)
    round_first(1)

    sends = [[] for _ in range(chunks)]
    flight, arrivals, staged = {}, {}, {}

    def remote(k, i, src, dst, dev):
        copy = pltpu.make_async_remote_copy(src_ref=src, dst_ref=dst, send_sem=send_sem.at[k, i],
                                            recv_sem=recv_sem.at[k, i], device_id=dev, device_id_type=MESH)
        copy.start()
        sends[k].append(copy)
        return copy

    def done_once(key):
        for copy in loads.pop(key, ()):
            copy.wait()

    cols_a, cols_b = pl.ds(0, CUT), pl.ds(CUT, width - CUT)
    bufs = {'f': (s32, k32, r32, x32, y32, 0), 'n': (s16, k16, r16, x16, y16, 5)}

    def send_partial(k, lhs, depth, weight, name):
        s_ref, k_ref, r_ref, _, _, i = bufs[name]

        def make(out, part):
            def tile(off, size):
                a = lhs[part * half:(part + 1) * half, :depth]
                b, cb = weight(off, size)
                out[k, :, :, :, pl.ds(off, size)] = dot(a, b, 1, cb).astype(out.dtype).reshape(2, 2, seq, size)
            tiles(width, 256, tile)
        make(s_ref, 1)
        flight[name, k] = [remote(k, i, s_ref.at[k], r_ref.at[k], core)]
        make(k_ref, 0)

    def chunk_of(buf, k):
        return buf[k].reshape(rows, width)

    def compute(t):
        h, k = divmod(t, chunks)
        mlp = h % 2 == 0
        if h > 0:
            for name, quad, nxt, buf, j in (('gn', quad_n, next_n, n_buf, 0), ('gg', quad_g, next_g, g_buf, 2)):
                first = local(quad.at[k], buf.at[k, 0], in_sem.at[k, j])
                arrivals.pop((name, k)).wait_recv()
                loads[name[1], k] = [first, local(nxt.at[k], buf.at[k, 1], in_sem.at[k, j + 1])]
            for copy in sends[k]:
                copy.wait_send()
            sends[k].clear()
        if k == 0:
            loads['w1' if mlp else 'w2'].wait()
        done_once(('n', k))
        if mlp:
            def up_tile(off, size):
                u = dot(chunk_of(n_buf, k), w1[:, pl.ds(off, size)], 1, 0)
                t_u = jnp.tanh(GELU_K * (u + 0.044715 * u * u * u))
                hid[k, :, pl.ds(off, size)] = (0.5 * u * (1.0 + t_u)).astype(BF)
                aux[:, pl.ds(off, size)] = 0.5 * (1.0 + t_u) + 0.5 * u * (1.0 - t_u * t_u) * (
                    GELU_K * (1.0 + 3 * 0.044715 * u * u))
            tiles(hid.shape[-1], 256, up_tile)
        else:
            def qkv_tile(off, size):
                hid[k, :, pl.ds(att_w + off, size)] = dot(chunk_of(n_buf, k), w2[pl.ds(off, size), :], 1, 1).astype(BF)
            tiles(3 * att_w, 256, qkv_tile)

            def fwd_seq(s, carry):
                r = pl.ds(pl.multiple_of(s * seq, seq), seq)
                for i in range(heads):
                    q, key, v = (hid[k, r, (j * heads + heads + i) * dim:(j * heads + heads + i + 1) * dim] for j in range(3))
                    scores = dot(q, key, 1, 1) * scale
                    expd = jnp.exp(scores - jnp.max(scores, axis=-1, keepdims=True))
                    prob = expd / jnp.sum(expd, axis=-1, keepdims=True)
                    aux[r, i * seq:(i + 1) * seq] = prob
                    hid[k, r, i * dim:(i + 1) * dim] = dot(prob.astype(BF), v, 1, 0).astype(BF)
                return carry
            lax.fori_loop(0, GROUP, fwd_seq, 0, unroll=4)
        if k == 0 and mlp:
            loads['w2'].wait()
        row0, depth = (0, hid.shape[-1]) if mlp else (3 * att_w, att_w)
        send_partial(k, hid.at[k], depth, lambda off, size: (w2[row0:row0 + depth, pl.ds(off, size)], 0), 'f')
        done_once(('g', k))
        if mlp:
            def down_tile(off, size):
                d_act = dot(chunk_of(g_buf, k), w2[pl.ds(off, size), :], 1, 1)
                dhid[k, :, pl.ds(off, size)] = (d_act * aux[:, pl.ds(off, size)]).astype(BF)
            tiles(dhid.shape[-1], 256, down_tile)
        else:
            dhid[k, :, 3 * att_w:4 * att_w] = dot(chunk_of(g_buf, k), w2[3 * att_w:, :], 1, 1).astype(BF)

            def bwd_seq(s, carry):
                r = pl.ds(pl.multiple_of(s * seq, seq), seq)
                for i in range(heads):
                    q, key, v = (hid[k, r, (j * heads + heads + i) * dim:(j * heads + heads + i + 1) * dim] for j in range(3))
                    prob = aux[r, i * seq:(i + 1) * seq]
                    d_out = dhid[k, r, 3 * att_w + i * dim:3 * att_w + (i + 1) * dim]
                    d_prob = dot(d_out, v, 1, 1).astype(BF).astype(F32)
                    row_dot = jnp.sum(d_prob * prob, axis=-1, keepdims=True)
                    d_score = (prob * (d_prob - row_dot) * scale).astype(BF)
                    parts = (dot(d_score, key, 1, 0), dot(d_score, q, 0, 0), dot(prob.astype(BF), d_out, 0, 0))
                    for j, part in enumerate(parts):
                        dhid[k, r, (j * heads + i) * dim:(j * heads + i + 1) * dim] = part.astype(BF)
                return carry
            lax.fori_loop(0, GROUP, bwd_seq, 0, unroll=4)
        if mlp:
            send_partial(k, dhid.at[k], dhid.shape[-1], lambda off, size: (w1[pl.ds(off, size), :], 1), 'n')
        else:
            send_partial(k, dhid.at[k], 3 * att_w, lambda off, size: (w2[:3 * att_w, pl.ds(off, size)], 0), 'n')
        if k == chunks - 1 and h + 1 < 2 * layers:
            load_weights(h + 1)
        core_done('f', t)
        core_done('n', t)

    def is_last(t):
        return t // chunks >= 2 * layers - 2

    def core_done(name, t):
        k = t % chunks
        _, kb, rb, xb, yb, i = bufs[name]
        flight[name, k][0].wait_recv()
        if is_last(t):
            flight[name, k][0].wait_send()
            sends[k] = [copy for copy in sends[k] if copy is not flight[name, k][0]]
        dt = kb.dtype
        for bx in (1, 0):
            for by in (1, 0):
                kb[k, bx, by] = (kb[k, bx, by].astype(F32) + rb[k, bx, by].astype(F32)).astype(dt)
        flight[name, k] = [remote(k, i + 1, kb.at[k, 1, :, :, cols_a], xb.at[k, :, :, cols_a], xax),
                           remote(k, i + 2, kb.at[k, :, 1, :, cols_b], xb.at[k, :, :, cols_b], yax)]

    def second_done(name, t):
        k = t % chunks
        _, kb, rb, xb, yb, i = bufs[name]
        dt = kb.dtype
        copy_a, copy_b = flight[name, k]
        copy_a.wait_recv()
        for j in (1, 0):
            kb[k, 0, j, :, :CUT] = (kb[k, 0, j, :, :CUT].astype(F32) + xb[k, j, :, :CUT].astype(F32)).astype(dt)
        third_a = remote(k, i + 3, kb.at[k, 0, 1, :, cols_a], yb.at[k, :, cols_a], yax)
        copy_b.wait_recv()
        for j in (1, 0):
            kb[k, j, 0, :, CUT:] = (kb[k, j, 0, :, CUT:].astype(F32) + xb[k, j, :, CUT:].astype(F32)).astype(dt)
        third_b = remote(k, i + 4, kb.at[k, 1, 0, :, cols_b], yb.at[k, :, cols_b], xax)
        flight[name, k] = [third_a, third_b]

    def quads(name, t):
        if is_last(t):
            return (s32, 10) if name == 'gn' else (r32, 15)
        return (quad_n, 10) if name == 'gn' else (quad_g, 15)

    def gather_start(name, t):
        k = t % chunks
        quad, i = quads(name, t)
        flight[name, k] = [
            remote(k, i, quad.at[k, 0, 0, :, cols_a], quad.at[k, 0, 1, :, cols_a], yax),
            remote(k, i + 1, quad.at[k, 0, 0, :, cols_b], quad.at[k, 1, 0, :, cols_b], xax)]

    def third_done(name, t):
        h, k = divmod(t, chunks)
        base, res, cot = (0, 1, 2) if h % 2 == 0 else (1, 0, 3)
        _, kb, rb, xb, yb, i = bufs[name]
        for copy in flight[name, k]:
            copy.wait_recv()
        summed = kb[k, 0, 0].astype(F32) + yb[k].astype(F32)
        for j in range(4):
            if ('own', j, k) in loads:
                loads.pop(('own', j, k)).wait()
        if name == 'f':
            value = own[res, k] - summed
            own[res, k] = value
            quad = quads('gn', t)[0]
            quad[k, 0, 0] = value if is_last(t) else rms_norm(value).astype(BF)
            gather_start('gn', t)
        else:
            x_in = own[base, k]
            inv = lax.rsqrt(jnp.mean(x_in * x_in, axis=-1, keepdims=True) + EPS)
            proj = jnp.mean(x_in * summed, axis=-1, keepdims=True)
            value = own[cot, k] + (inv * summed - x_in * (inv * inv * inv * proj))
            own[cot, k] = value
            quad = quads('gg', t)[0]
            quad[k, 0, 0] = value.astype(quad.dtype)
            gather_start('gg', t)

    def gather_second(name, t):
        k = t % chunks
        quad, i = quads(name, t)
        copy_a, copy_b = flight[name, k]
        copy_a.wait_recv()
        second_a = remote(k, i + 2, quad.at[k, 0, :, :, cols_a], quad.at[k, 1, :, :, cols_a], xax)
        copy_b.wait_recv()
        second_b = remote(k, i + 3, quad.at[k, :, 0, :, cols_b], quad.at[k, :, 1, :, cols_b], yax)
        flight[name, k] = [second_a, second_b]

    finals = []

    def gather_core(t):
        h, k = divmod(t, chunks)
        more = h + 1 < 2 * layers
        for name in ('gn', 'gg'):
            for copy in flight[name, k]:
                copy.wait_recv()
        if is_last(t):
            leaving = []
            outs = (x2, dx1) if h % 2 == 0 else (x1, dx2)
            for j, (name, out) in enumerate(zip(('gn', 'gg'), outs)):
                quad = quads(name, t)[0]
                for b in range(4):
                    bx, by = divmod(b, 2)
                    there = place(k, 0, bx, by)
                    far = pltpu.make_async_remote_copy(
                        src_ref=quad.at[k, bx, by], dst_ref=out.at[there], send_sem=fsend_sem.at[k, 4 * j + b],
                        recv_sem=frecv_sem.at[k, 4 * j + b], device_id=core, device_id_type=MESH)
                    far.start()
                    leaving.append((far, local(quad.at[k, bx, by], out.at[there], out_sem.at[k, 4 * j + b])))
            if more:
                for b in range(4):
                    bx, by = divmod(b, 2)
                    quad_n[k, bx, by] = rms_norm(s32[k, bx, by]).astype(BF)
                    quad_g[k, bx, by] = r32[k, bx, by].astype(BF)
                for far, near in leaving:
                    far.wait()
                    near.wait()
                for copy in sends[k]:
                    copy.wait_send()
                sends[k].clear()
            else:
                finals.extend(leaving)
        if more:
            arrivals['gn', k] = remote(k, 14, quad_n.at[k], next_n.at[k], core)
            arrivals['gg', k] = remote(k, 19, quad_g.at[k], next_g.at[k], core)

    def stage(slot, shape, dst):
        return pltpu.make_async_copy(aux.at[pl.ds(slot * 256, shape[0]), pl.ds(0, shape[1])], dst, wg_sem.at[slot])

    def weight_grads(h):
        layer = layers - 1 - h // 2
        mlp = h % 2 == 0
        total = chunks * rows

        def put(slot, value, dst, wait):
            copy = stage(slot, value.shape, dst)
            if wait is None:
                copy.wait()
            else:
                @pl.when(wait)
                def _():
                    copy.wait()
            aux[slot * 256:slot * 256 + value.shape[0], :value.shape[1]] = value
            copy.start()

        def wide(lhs, rhs, out, row0, lo, hi):
            def body(i, carry):
                off = pl.multiple_of(i * 256, 256)
                a = lhs[:, :, pl.ds(off, 256)].reshape(total, 256)
                for slot, (c0, cw) in enumerate(((0, CUT), (CUT, width - CUT))):
                    b = rhs[:, :, :, :, :, c0:c0 + cw].reshape(total, cw)
                    put(slot, dot(a, b, 0, 0), out.at[layer, pl.ds(row0 + off, 256), pl.ds(c0, cw)], i > lo)
                return carry
            lax.fori_loop(lo, hi, body, 0)
            for slot, (c0, cw) in enumerate(((0, CUT), (CUT, width - CUT))):
                stage(slot, (256, cw), out.at[layer, pl.ds(row0, 256), pl.ds(c0, cw)]).wait()

        def tall(lo, hi, size=256):
            cw = dhid.shape[-1] // 2

            def body(i, carry):
                off = i * 256 if size != 256 else pl.multiple_of(i * 256, 256)
                a = n_buf[:, :, :, :, :, pl.ds(off, size)].reshape(total, size)
                for slot in range(2):
                    b = dhid[:, :, slot * cw:(slot + 1) * cw].reshape(total, cw)
                    put(slot, dot(a, b, 0, 0), dwu.at[layer, pl.ds(off, size), pl.ds(slot * cw, cw)], i > lo)
                return carry
            if size == 256:
                lax.fori_loop(lo, hi, body, 0)
            else:
                body(lo, 0)
            for slot in range(2):
                stage(slot, (size, cw), dwu.at[layer, pl.ds(0, size), pl.ds(slot * cw, cw)]).wait()

        if not mlp:
            cut = 3 * att_w // 512
            return [lambda: wide(dhid, n_buf, dwa, 0, 0, cut), lambda: wide(dhid, n_buf, dwa, 0, cut, 3 * att_w // 256),
                    lambda: wide(hid, g_buf, dwa, 3 * att_w, 0, att_w // 256)]
        deep, high = hid.shape[-1] // 256, width // 256
        pieces = [lambda: wide(hid, g_buf, dwd, 0, 0, deep // 2), lambda: wide(hid, g_buf, dwd, 0, deep // 2, deep),
                  lambda: tall(0, high // 2), lambda: tall(high // 2, high)]
        if width % 256:
            pieces.append(lambda: tall(high, high, width % 256))
        return pieces

    tasks = 2 * layers * chunks
    for t in range(tasks + 2):
        pieces = []
        if t == 1:
            for i in range(2, len(firsts)):
                round_first(i)
        if t < tasks:
            compute(t)
            if t % chunks == chunks - 1:
                pieces = weight_grads(t // chunks)
        if 0 <= t - 1 < tasks:
            third_done('f', t - 1)
            third_done('n', t - 1)
        for piece in pieces[:2]:
            piece()
        if 0 <= t - 2 < tasks:
            gather_core(t - 2)
        for piece in pieces[2:3]:
            piece()
        if t < tasks:
            second_done('f', t)
            second_done('n', t)
        if 0 <= t - 1 < tasks:
            gather_second('gn', t - 1)
            gather_second('gg', t - 1)
        for piece in pieces[3:]:
            piece()
    for far, near in finals:
        far.wait()
        near.wait()
    for k in range(chunks):
        for copy in sends[k]:
            copy.wait_send()


def run_stack(acts, w_att, w_up, w_down, heads, scale):
    layers, width, hid = w_up.shape
    att_w = w_att.shape[1] // 4
    seq = acts[0].shape[1]
    chunks = acts[0].shape[0] // GROUP
    rows = GROUP * seq
    quad = (chunks, 2, 2, seq, width)
    oct_ = (chunks, 2, 2, 2, seq, width)
    scratch = [pltpu.VMEM(oct_, BF), pltpu.VMEM(oct_, BF), pltpu.VMEM((width, hid), BF), pltpu.VMEM((hid, width), BF),
               pltpu.VMEM((4, chunks, seq, width), F32),
               pltpu.VMEM((chunks, rows, hid), BF), pltpu.VMEM((chunks, rows, hid), BF),
               pltpu.VMEM((rows, hid), F32)]
    for dt in (F32, BF):
        scratch += [pltpu.VMEM(quad, dt)] * 3
        scratch += [pltpu.VMEM((chunks, 2, seq, width), dt), pltpu.VMEM((chunks, seq, width), dt)]
    scratch += [pltpu.VMEM(quad, BF)] * 2
    dma = pltpu.SemaphoreType.DMA
    scratch += [dma((chunks, 4)), dma((2, 8)), dma((chunks, 4)), dma((2,)), dma((2,)), dma((chunks, 8)),
                dma((chunks, 20)), dma((chunks, 20)), dma((chunks, 8)), dma((chunks, 8))]
    any_spec = pl.BlockSpec(memory_space=pl.ANY)
    outs = [jax.ShapeDtypeStruct(a.shape, F32) for a in acts]
    outs += [jax.ShapeDtypeStruct(w.shape, F32) for w in (w_att, w_up, w_down)]
    outs += [jax.ShapeDtypeStruct(quad, BF)] * 2
    return pl.pallas_call(
        functools.partial(backward_pass, layers, chunks, seq, heads, att_w // heads, scale),
        out_shape=outs,
        in_specs=[any_spec] * 7,
        out_specs=[any_spec] * 9,
        scratch_shapes=scratch,
        compiler_params=pltpu.CompilerParams(collective_id=0, has_side_effects=True, vmem_limit_bytes=VMEM_LIMIT),
        name='backward_pass',
    )(*acts, w_att, w_up, w_down)


def copy_out(heads_att, head_dim, *refs):
    ins, outs = refs[:7], refs[7:]
    for src, dst in zip(ins[:6], outs[:6]):
        dst[...] = src[...]
    place = lax.rem(pl.program_id(0), heads_att)
    dq, do = outs[6:]

    @pl.when(place < 3 * heads_att // 4)
    def _():
        dq[...] = ins[6][:, :head_dim]

    @pl.when(place >= 3 * heads_att // 4)
    def _():
        do[...] = ins[6][:, :head_dim]


def write_results(acts, dwu, dwd, dwa, heads, head_dim):
    steps, seq, width = acts[0].shape
    layers = dwu.shape[0]
    per = steps // layers
    each = 4 * heads
    dwa = dwa.reshape(layers * each, -1, width)

    def split(a):
        return a.reshape(steps, -1, a.shape[-1])
    arrays = [*acts, split(dwu), split(dwd), dwa]

    def whole(a):
        return pl.BlockSpec((1,) + a.shape[1:], lambda i: (i, 0, 0))
    q_spec = pl.BlockSpec((1, head_dim, width), lambda i: (i // each * 3 * heads + jnp.minimum(i % each, 3 * heads - 1), 0, 0))
    o_spec = pl.BlockSpec((1, head_dim, width), lambda i: (i // each * heads + jnp.maximum(i % each - 3 * heads, 0), 0, 0))
    outs = pl.pallas_call(
        functools.partial(copy_out, each, head_dim),
        grid=(steps,),
        in_specs=[whole(a) for a in arrays],
        out_specs=[whole(a) for a in arrays[:6]] + [q_spec, o_spec],
        out_shape=[jax.ShapeDtypeStruct(a.shape, F32) for a in arrays[:6]] + [
            jax.ShapeDtypeStruct((layers * 3 * heads, head_dim, width), F32),
            jax.ShapeDtypeStruct((layers * heads, head_dim, width), F32)],
        compiler_params=pltpu.CompilerParams(vmem_limit_bytes=VMEM_LIMIT),
        name='write_results',
    )(*arrays)
    return (*outs[:4], outs[4].reshape(dwu.shape), outs[5].reshape(dwd.shape),
            outs[6].reshape(layers, 3, heads, head_dim, width), outs[7].reshape(layers, heads, head_dim, width))


def solution(mesh):
    act_spec = P('dp')
    in_specs = (act_spec, act_spec, act_spec, act_spec,
                P(None, None, None, 'tp', None), P(None, 'tp', None, None),
                P(None, None, 'tp'), P(None, 'tp', None))
    out_specs = (act_spec, act_spec, act_spec, act_spec,
                 P('dp', None, None, 'tp', None), P('dp', 'tp', None, None),
                 P('dp', None, 'tp'), P('dp', 'tp', None))

    def device_body(y_one, y_two, dy_one, dy_two, w_qkv, w_out, w_up, w_down):
        n_micro, n_batch, seq, width = y_one.shape
        layers, heads, head_dim = w_qkv.shape[0], w_qkv.shape[3], w_qkv.shape[4]
        pad = -head_dim % 128
        pdim = head_dim + pad
        chunks = n_micro * n_batch // GROUP
        acts = [a.reshape(chunks * GROUP, seq, width) for a in (y_one, y_two, dy_one, dy_two)]
        w_q = jnp.pad(w_qkv.transpose(0, 2, 3, 4, 1).reshape(layers, 3 * heads, head_dim, width), ((0, 0), (0, 0), (0, pad), (0, 0)))
        w_o = jnp.pad(w_out, ((0, 0), (0, 0), (0, pad), (0, 0)))
        w_att = jnp.concatenate([w_q, w_o], axis=1).reshape(layers, 4 * heads * pdim, width)
        x1, x2, dx1, dx2, dwa, dwu, dwd, _, _ = run_stack(acts, w_att, w_up, w_down, heads, head_dim ** -0.5)
        x1, x2, dx1, dx2, dwu, dwd, dwq, dwo = write_results((x1, x2, dx1, dx2), dwu, dwd, dwa, heads, head_dim)
        return (*(a.reshape(y_one.shape) for a in (x1, x2, dx1, dx2)), dwq.transpose(0, 4, 1, 2, 3), dwo, dwu, dwd)

    return jax.shard_map(device_body, mesh=mesh, in_specs=in_specs, out_specs=out_specs, check_vma=False)
```

time: 1640 us -> 922 us (0.56)
  waiting for transfers between devices: 1020 us -> 0 us
  Pallas kernels: 0 us -> 902 us
  matrix products: 359 us -> 0 us
  other arithmetic: 195 us -> 10.1 us
  local copies, waits for them, and re-layouts: 25.7 us -> 0 us
    psum x12 -> x0, waiting for transfers between devices: 1020 us -> none  [the longest x3 415 us: device_body(): lower_one = upper_one - lax.psum(f_part, 'tp')]
    pallas_call x0 -> x2, Pallas kernels: none -> 902 us  [the longest x1 836 us: run_stack(): pl.pallas_call(functools.partial(backward_pass, layers, chunks, seq, head...]
    dot_general x51 -> x0, matrix products: 349 us -> none  [the longest x3 44.2 us: mlp_backward(): jnp.einsum('rsh,fh->rsf', grad_half, w_down, preferred_element_type=jnp.f...]
    reduce_sum x11 -> x0, other arithmetic: 114 us -> none  [rms_norm(): return x_in * lax.rsqrt(jnp.mean(x_in * x_in, axis=-1, keepdims=True) + EPS)]
    add x4 -> x0, other arithmetic: 34.2 us -> none  [the longest x2 22.2 us: device_body(): grad_one = grad_one + norm_back(upper_one, norm_sum.astype(jnp.float32))]
    another operation x4 -> x0, other arithmetic: 33.9 us -> none  [the longest x1 16 us: device_body(): jnp.stack(grads_down[::-1])]
    unnamed x154 -> x0, local copies, waits for them, and re-layouts: 25.7 us -> none
  transfers between devices with their start and end apart: 12 -> 0, of which waited for: 12 -> 0; matrix products, arithmetic and copies ran while one was open for 19% -> 0% of each run, Pallas kernels for 0% -> 0%
where the time goes in v2:
time: 922 us; the launch traced here: 913 us
  Pallas kernels  902 us (98%)
  other arithmetic  10.1 us (1%)
    pallas_call x1, Pallas kernels, run_stack(): pl.pallas_call(functools.partial(backward_pass, layers, chunks, seq, head...  836 us
    pallas_call x1, Pallas kernels, write_results(): pl.pallas_call(functools.partial(copy_out, each, head_dim), grid=(steps,)...  66 us

profile of v2, /device:TPU:0, one launch (start us, length us, event | category | flops | bytes accessed | tf_op | source)
XLA Modules:
  0.0 912.8 jit_solution(4482043804786268532)
XLA Ops:
  0.6 10.1 %fusion.2 = bf16[3,8,128,1664]{3,2,1,0:T(8,128)(2,1)} fusion(bf16[3,2,104,1664]{3,2,1,0:T(8,128)(2,1)} %param.13, bf16[3,6,104,1664]{3,2,1,0:T(8,128)(2,1)} %bitcast.29), kind=kLoop, calls=%fused_computation.4 | loop fusion | flops 40894464 | bytes 18530304 | tf_op jit(solution)/shard_map/concatenate | solution.py:527
  10.7 835.6 %backward_pass.1 = (f32[24,64,1664]{2,1,0:T(8,128)}, f32[24,64,1664]{2,1,0:T(8,128)}, f32[24,64,1664]{2,1,0:T(8,128)}, f32[24,64,1664]{2,1,0:T(8,128)}, f32[3,10...) custom-call(f32[24,64,1664]{2,1,0:T(8,128)} %bitcast.25, ...), custom_call_target="tpu_custom_call" | custom-call | tf_op jit(solution)/shard_map/backward_pass/pallas_call | solution.py:452
  846.3 66.0 %write_results.1 = (f32[24,64,1664]{2,1,0:T(8,128)}, f32[24,64,1664]{2,1,0:T(8,128)}, f32[24,64,1664]{2,1,0:T(8,128)}, f32[24,64,1664]{2,1,0:T(8,128)}, f32[24,2...) custom-call(f32[24,64,1664]{2,1,0:T(8,128)} %get-tuple-element.23.refs_0_, ...), custom_call_target="tpu_custom_call" | custom-call | tf_op jit(solution)/shard_map/write_results/pallas_call | solution.py:494

commit v3 on v2

--- a/solution.py
+++ b/solution.py
@@ -174,7 +174,7 @@
                     scores = dot(q, key, 1, 1) * scale
                     expd = jnp.exp(scores - jnp.max(scores, axis=-1, keepdims=True))
                     prob = expd / jnp.sum(expd, axis=-1, keepdims=True)
-                    aux[r, i * seq:(i + 1) * seq] = prob
+                    aux[r, i * 128:i * 128 + seq] = prob
                     hid[k, r, i * dim:(i + 1) * dim] = dot(prob.astype(BF), v, 1, 0).astype(BF)
                 return carry
             lax.fori_loop(0, GROUP, fwd_seq, 0, unroll=4)
@@ -195,7 +195,7 @@
                 r = pl.ds(pl.multiple_of(s * seq, seq), seq)
                 for i in range(heads):
                     q, key, v = (hid[k, r, (j * heads + heads + i) * dim:(j * heads + heads + i + 1) * dim] for j in range(3))
-                    prob = aux[r, i * seq:(i + 1) * seq]
+                    prob = aux[r, i * 128:i * 128 + seq]
                     d_out = dhid[k, r, 3 * att_w + i * dim:3 * att_w + (i + 1) * dim]
                     d_prob = dot(d_out, v, 1, 1).astype(BF).astype(F32)
                     row_dot = jnp.sum(d_prob * prob, axis=-1, keepdims=True)
@@ -205,14 +205,15 @@
                         dhid[k, r, (j * heads + i) * dim:(j * heads + i + 1) * dim] = part.astype(BF)
                 return carry
             lax.fori_loop(0, GROUP, bwd_seq, 0, unroll=4)
-        if mlp:
+
+    def compute_rest(t):
+        h, k = divmod(t, chunks)
+        if h % 2 == 0:
             send_partial(k, dhid.at[k], dhid.shape[-1], lambda off, size: (w1[pl.ds(off, size), :], 1), 'n')
         else:
             send_partial(k, dhid.at[k], 3 * att_w, lambda off, size: (w2[:3 * att_w, pl.ds(off, size)], 0), 'n')
         if k == chunks - 1 and h + 1 < 2 * layers:
             load_weights(h + 1)
-        core_done('f', t)
-        core_done('n', t)
 
     def is_last(t):
         return t // chunks >= 2 * layers - 2
@@ -397,26 +398,33 @@
         if t == 1:
             for i in range(2, len(firsts)):
                 round_first(i)
-        if t < tasks:
+        now, one_ago, two_ago = (0 <= i < tasks for i in (t, t - 1, t - 2))
+        if now:
             compute(t)
+            core_done('f', t)
             if t % chunks == chunks - 1:
                 pieces = weight_grads(t // chunks)
-        if 0 <= t - 1 < tasks:
+        if one_ago:
             third_done('f', t - 1)
             third_done('n', t - 1)
-        for piece in pieces[:2]:
+        if now:
+            compute_rest(t)
+        if two_ago:
+            gather_core(t - 2)
+        if now:
+            core_done('n', t)
+        for piece in pieces[:1]:
             piece()
-        if 0 <= t - 2 < tasks:
-            gather_core(t - 2)
-        for piece in pieces[2:3]:
+        if now:
+            second_done('f', t)
+        for piece in pieces[1:2]:
             piece()
-        if t < tasks:
-            second_done('f', t)
+        if now:
             second_done('n', t)
-        if 0 <= t - 1 < tasks:
+        if one_ago:
             gather_second('gn', t - 1)
             gather_second('gg', t - 1)
-        for piece in pieces[3:]:
+        for piece in pieces[2:]:
             piece()
     for far, near in finals:
         far.wait()

time: 922 us -> 896 us (0.972)
  Pallas kernels: 902 us -> 876 us
    pallas_call x1, Pallas kernels: 836 us -> 809 us  [run_stack(): pl.pallas_call(functools.partial(backward_pass, layers, chunks, seq, head...]
where the time goes in v3:
time: 896 us; the launch traced here: 887 us
  Pallas kernels  876 us (98%)
  other arithmetic  10.1 us (1%)
    pallas_call x1, Pallas kernels, run_stack(): pl.pallas_call(functools.partial(backward_pass, layers, chunks, seq, head...  809 us
    pallas_call x1, Pallas kernels, write_results(): pl.pallas_call(functools.partial(copy_out, each, head_dim), grid=(steps,)...  66 us

profile of v3, /device:TPU:0, one launch (start us, length us, event | category | flops | bytes accessed | tf_op | source)
XLA Modules:
  0.0 886.7 jit_solution(8657134087728970742)
XLA Ops:
  0.6 10.1 %fusion.2 = bf16[3,8,128,1664]{3,2,1,0:T(8,128)(2,1)} fusion(bf16[3,2,104,1664]{3,2,1,0:T(8,128)(2,1)} %param.13, bf16[3,6,104,1664]{3,2,1,0:T(8,128)(2,1)} %bitcast.29), kind=kLoop, calls=%fused_computation.4 | loop fusion | flops 40894464 | bytes 18530304 | tf_op jit(solution)/shard_map/concatenate | solution.py:535
  10.7 809.5 %backward_pass.1 = (f32[24,64,1664]{2,1,0:T(8,128)}, f32[24,64,1664]{2,1,0:T(8,128)}, f32[24,64,1664]{2,1,0:T(8,128)}, f32[24,64,1664]{2,1,0:T(8,128)}, f32[3,10...) custom-call(f32[24,64,1664]{2,1,0:T(8,128)} %bitcast.25, ...), custom_call_target="tpu_custom_call" | custom-call | tf_op jit(solution)/shard_map/backward_pass/pallas_call | solution.py:460
  820.2 66.0 %write_results.1 = (f32[24,64,1664]{2,1,0:T(8,128)}, f32[24,64,1664]{2,1,0:T(8,128)}, f32[24,64,1664]{2,1,0:T(8,128)}, f32[24,64,1664]{2,1,0:T(8,128)}, f32[24,2...) custom-call(f32[24,64,1664]{2,1,0:T(8,128)} %get-tuple-element.23.refs_0_, ...), custom_call_target="tpu_custom_call" | custom-call | tf_op jit(solution)/shard_map/write_results/pallas_call | solution.py:502

commit v4 on v3

--- a/solution.py
+++ b/solution.py
@@ -105,7 +105,6 @@
             loads['own', j, k] = local(src.at[k * GROUP + mine], own.at[j, k], own_sem.at[k, j])
     pl.semaphore_wait(barrier, 3)
     round_first(0)
-    round_first(1)
 
     sends = [[] for _ in range(chunks)]
     flight, arrivals, staged = {}, {}, {}
@@ -140,17 +139,20 @@
     def chunk_of(buf, k):
         return buf[k].reshape(rows, width)
 
-    def compute(t):
+    def prefetch(t):
         h, k = divmod(t, chunks)
-        mlp = h % 2 == 0
         if h > 0:
             for name, quad, nxt, buf, j in (('gn', quad_n, next_n, n_buf, 0), ('gg', quad_g, next_g, g_buf, 2)):
                 first = local(quad.at[k], buf.at[k, 0], in_sem.at[k, j])
                 arrivals.pop((name, k)).wait_recv()
                 loads[name[1], k] = [first, local(nxt.at[k], buf.at[k, 1], in_sem.at[k, j + 1])]
-            for copy in sends[k]:
-                copy.wait_send()
-            sends[k].clear()
+
+    def compute(t):
+        h, k = divmod(t, chunks)
+        mlp = h % 2 == 0
+        for copy in sends[k]:
+            copy.wait_send()
+        sends[k].clear()
         if k == 0:
             loads['w1' if mlp else 'w2'].wait()
         done_once(('n', k))
@@ -182,6 +184,8 @@
             loads['w2'].wait()
         row0, depth = (0, hid.shape[-1]) if mlp else (3 * att_w, att_w)
         send_partial(k, hid.at[k], depth, lambda off, size: (w2[row0:row0 + depth, pl.ds(off, size)], 0), 'f')
+        if t == 0:
+            round_first(1)
         done_once(('g', k))
         if mlp:
             def down_tile(off, size):
@@ -256,8 +260,8 @@
         k = t % chunks
         quad, i = quads(name, t)
         flight[name, k] = [
-            remote(k, i, quad.at[k, 0, 0, :, cols_a], quad.at[k, 0, 1, :, cols_a], yax),
-            remote(k, i + 1, quad.at[k, 0, 0, :, cols_b], quad.at[k, 1, 0, :, cols_b], xax)]
+            remote(k, i, quad.at[k, 0, 0, :, cols_a], quad.at[k, 1, 0, :, cols_a], xax),
+            remote(k, i + 1, quad.at[k, 0, 0, :, cols_b], quad.at[k, 0, 1, :, cols_b], yax)]
 
     def third_done(name, t):
         h, k = divmod(t, chunks)
@@ -290,9 +294,9 @@
         quad, i = quads(name, t)
         copy_a, copy_b = flight[name, k]
         copy_a.wait_recv()
-        second_a = remote(k, i + 2, quad.at[k, 0, :, :, cols_a], quad.at[k, 1, :, :, cols_a], xax)
+        second_a = remote(k, i + 2, quad.at[k, :, 0, :, cols_a], quad.at[k, :, 1, :, cols_a], yax)
         copy_b.wait_recv()
-        second_b = remote(k, i + 3, quad.at[k, :, 0, :, cols_b], quad.at[k, :, 1, :, cols_b], yax)
+        second_b = remote(k, i + 3, quad.at[k, 0, :, :, cols_b], quad.at[k, 1, :, :, cols_b], xax)
         flight[name, k] = [second_a, second_b]
 
     finals = []
@@ -393,6 +397,7 @@
         return pieces
 
     tasks = 2 * layers * chunks
+    early = set()
     for t in range(tasks + 2):
         pieces = []
         if t == 1:
@@ -404,7 +409,7 @@
             core_done('f', t)
             if t % chunks == chunks - 1:
                 pieces = weight_grads(t // chunks)
-        if one_ago:
+        if one_ago and t - 1 not in early:
             third_done('f', t - 1)
             third_done('n', t - 1)
         if now:
@@ -421,11 +426,21 @@
             piece()
         if now:
             second_done('n', t)
+        if t + 1 < tasks and not pieces:
+            prefetch(t + 1)
         if one_ago:
             gather_second('gn', t - 1)
             gather_second('gg', t - 1)
-        for piece in pieces[2:]:
+        for piece in pieces[2:4]:
             piece()
+        if len(pieces) > 4:
+            third_done('f', t)
+            third_done('n', t)
+            early.add(t)
+        for piece in pieces[4:]:
+            piece()
+        if t + 1 < tasks and pieces:
+            prefetch(t + 1)
     for far, near in finals:
         far.wait()
         near.wait()

time: 896 us -> 880 us (0.982)
  Pallas kernels: 876 us -> 860 us
    pallas_call x1, Pallas kernels: 809 us -> 794 us  [run_stack(): pl.pallas_call(functools.partial(backward_pass, layers, chunks, seq, head...]
where the time goes in v4:
time: 880 us; the launch traced here: 871 us
  Pallas kernels  860 us (98%)
  other arithmetic  10.1 us (1%)
    pallas_call x1, Pallas kernels, run_stack(): pl.pallas_call(functools.partial(backward_pass, layers, chunks, seq, head...  794 us
    pallas_call x1, Pallas kernels, write_results(): pl.pallas_call(functools.partial(copy_out, each, head_dim), grid=(steps,)...  66 us

profile of v4, /device:TPU:0, one launch (start us, length us, event | category | flops | bytes accessed | tf_op | source)
XLA Modules:
  0.0 871.4 jit_solution(5641163637774547048)
XLA Ops:
  0.6 10.1 %fusion.2 = bf16[3,8,128,1664]{3,2,1,0:T(8,128)(2,1)} fusion(bf16[3,2,104,1664]{3,2,1,0:T(8,128)(2,1)} %param.13, bf16[3,6,104,1664]{3,2,1,0:T(8,128)(2,1)} %bitcast.29), kind=kLoop, calls=%fused_computation.4 | loop fusion | flops 40894464 | bytes 18530304 | tf_op jit(solution)/shard_map/concatenate | solution.py:550
  10.7 794.2 %backward_pass.1 = (f32[24,64,1664]{2,1,0:T(8,128)}, f32[24,64,1664]{2,1,0:T(8,128)}, f32[24,64,1664]{2,1,0:T(8,128)}, f32[24,64,1664]{2,1,0:T(8,128)}, f32[3,10...) custom-call(f32[24,64,1664]{2,1,0:T(8,128)} %bitcast.25, ...), custom_call_target="tpu_custom_call" | custom-call | tf_op jit(solution)/shard_map/backward_pass/pallas_call | solution.py:475
  804.9 66.0 %write_results.1 = (f32[24,64,1664]{2,1,0:T(8,128)}, f32[24,64,1664]{2,1,0:T(8,128)}, f32[24,64,1664]{2,1,0:T(8,128)}, f32[24,64,1664]{2,1,0:T(8,128)}, f32[24,2...) custom-call(f32[24,64,1664]{2,1,0:T(8,128)} %get-tuple-element.23.refs_0_, ...), custom_call_target="tpu_custom_call" | custom-call | tf_op jit(solution)/shard_map/write_results/pallas_call | solution.py:517

commit v5 on v4

--- a/solution.py
+++ b/solution.py
@@ -414,23 +414,24 @@
             third_done('n', t - 1)
         if now:
             compute_rest(t)
+        if now:
+            core_done('n', t)
         if two_ago:
             gather_core(t - 2)
-        if now:
-            core_done('n', t)
         for piece in pieces[:1]:
             piece()
         if now:
             second_done('f', t)
         for piece in pieces[1:2]:
             piece()
+        if one_ago:
+            gather_second('gn', t - 1)
         if now:
             second_done('n', t)
+        if one_ago:
+            gather_second('gg', t - 1)
         if t + 1 < tasks and not pieces:
             prefetch(t + 1)
-        if one_ago:
-            gather_second('gn', t - 1)
-            gather_second('gg', t - 1)
         for piece in pieces[2:4]:
             piece()
         if len(pieces) > 4:

time: 880 us -> 884 us (level)
  no operation moved by 1% of the time
where the time goes in v5:
time: 884 us; the launch traced here: 875 us
  Pallas kernels  864 us (98%)
  other arithmetic  10.1 us (1%)
    pallas_call x1, Pallas kernels, run_stack(): pl.pallas_call(functools.partial(backward_pass, layers, chunks, seq, head...  797 us
    pallas_call x1, Pallas kernels, write_results(): pl.pallas_call(functools.partial(copy_out, each, head_dim), grid=(steps,)...  66 us

profile of v5, /device:TPU:0, one launch (start us, length us, event | category | flops | bytes accessed | tf_op | source)
XLA Modules:
  0.0 874.7 jit_solution(4776882652262964217)
XLA Ops:
  0.6 10.1 %fusion.2 = bf16[3,8,128,1664]{3,2,1,0:T(8,128)(2,1)} fusion(bf16[3,2,104,1664]{3,2,1,0:T(8,128)(2,1)} %param.13, bf16[3,6,104,1664]{3,2,1,0:T(8,128)(2,1)} %bitcast.29), kind=kLoop, calls=%fused_computation.4 | loop fusion | flops 40894464 | bytes 18530304 | tf_op jit(solution)/shard_map/concatenate | solution.py:551
  10.7 797.5 %backward_pass.1 = (f32[24,64,1664]{2,1,0:T(8,128)}, f32[24,64,1664]{2,1,0:T(8,128)}, f32[24,64,1664]{2,1,0:T(8,128)}, f32[24,64,1664]{2,1,0:T(8,128)}, f32[3,10...) custom-call(f32[24,64,1664]{2,1,0:T(8,128)} %bitcast.25, ...), custom_call_target="tpu_custom_call" | custom-call | tf_op jit(solution)/shard_map/backward_pass/pallas_call | solution.py:476
  808.2 66.0 %write_results.1 = (f32[24,64,1664]{2,1,0:T(8,128)}, f32[24,64,1664]{2,1,0:T(8,128)}, f32[24,64,1664]{2,1,0:T(8,128)}, f32[24,64,1664]{2,1,0:T(8,128)}, f32[24,2...) custom-call(f32[24,64,1664]{2,1,0:T(8,128)} %get-tuple-element.23.refs_0_, ...), custom_call_target="tpu_custom_call" | custom-call | tf_op jit(solution)/shard_map/write_results/pallas_call | solution.py:518
